TPU v7x, 32 devices: a 4x4x1 block of a 4x4x8 slice. The times are simulated.
32 devices in a mesh: rep: 1 (over z), dp: 4 (over y), sp: 8 (over x, core).
Axes of the slice: x: 4, y: 4, z: 1, core: 2. Of those that a mesh axis runs over, the one named last changes fastest.
The devices are a block of a 4x4x8 slice.
Arguments:
- hidden: bfloat16 [256, 4096], P(('rep', 'dp'))
- w_query: bfloat16 [4096, 4096], replicated
- w_key: bfloat16 [4096, 256], replicated
- w_value: bfloat16 [4096, 256], replicated
- w_out: bfloat16 [4096, 4096], P('sp')
- k_cache: bfloat16 [256, 2048, 1, 256], P(('rep', 'dp'), 'sp')
- v_cache: bfloat16 [256, 2048, 1, 256], P(('rep', 'dp'), 'sp')
- write_pos: int32 [256], P(('rep', 'dp'))
- valid_len: int32 [256], P(('rep', 'dp'))
Outputs:
- output 1: bfloat16 [256, 4096], P(('rep', 'dp'))
- output 2: bfloat16 [256, 2048, 1, 256], P(('rep', 'dp'), 'sp')
- output 3: bfloat16 [256, 2048, 1, 256], P(('rep', 'dp'), 'sp')
All inputs are finite; a program needn't handle non-finite values.
Results may differ from a plain program's by a relative error of at most 0.00650376.
Values are sent between devices in bfloat16 or wider.
A program may use at most 768 MiB of HBM per device.

v0:
```python
import jax
import jax.numpy as jnp
from jax import lax
from jax.sharding import PartitionSpec as P

NEG_FLOOR = -1e30


def solution(mesh):
    row_spec = P(('rep', 'dp'), None)
    cache_spec = P(('rep', 'dp'), 'sp', None, None)
    len_spec = P(('rep', 'dp'))

    def local_step(hidden, w_query, w_key, w_value, w_out, k_cache, v_cache, write_pos, valid_len):
        num_rows, seq_local, kv_heads, head_dim = k_cache.shape
        num_heads = w_query.shape[1] // head_dim
        group_size = num_heads // kv_heads
        shard_idx = lax.axis_index('sp')
        query = jnp.dot(hidden, w_query, preferred_element_type=jnp.float32).astype(jnp.bfloat16)
        query = query.reshape(num_rows, kv_heads, group_size, head_dim)
        key_new = jnp.dot(hidden, w_key, preferred_element_type=jnp.float32).astype(jnp.bfloat16)
        value_new = jnp.dot(hidden, w_value, preferred_element_type=jnp.float32).astype(jnp.bfloat16)
        positions = shard_idx * seq_local + jnp.arange(seq_local, dtype=jnp.int32)
        at_pos = (positions[None, :] == write_pos[:, None])[:, :, None, None]
        k_next = jnp.where(at_pos, key_new.reshape(num_rows, 1, kv_heads, head_dim), k_cache)
        v_next = jnp.where(at_pos, value_new.reshape(num_rows, 1, kv_heads, head_dim), v_cache)
        scores = jnp.einsum('bkgd,bskd->bkgs', query, k_next, preferred_element_type=jnp.float32) * head_dim ** -0.5
        valid_mask = (positions[None, :] < valid_len[:, None])[:, None, None, :]
        scores = jnp.where(valid_mask, scores, -jnp.inf)
        local_max = jnp.maximum(jnp.max(scores, axis=-1), NEG_FLOOR)
        weights = jnp.exp(scores - local_max[..., None])
        local_sum = jnp.sum(weights, axis=-1)
        local_acc = jnp.einsum('bkgs,bskd->bkgd', weights.astype(jnp.bfloat16), v_next, preferred_element_type=jnp.float32)
        global_max = lax.pmax(local_max, 'sp')
        rescale = jnp.exp(local_max - global_max)
        packed = jnp.concatenate([local_acc * rescale[..., None], (local_sum * rescale)[..., None]], axis=-1)
        packed = lax.psum(packed, 'sp')
        attention = (packed[..., :head_dim] / packed[..., head_dim:]).astype(jnp.bfloat16)
        attention = attention.reshape(num_rows, num_heads * head_dim)
        out_rows = w_out.shape[0]
        attn_mine = lax.dynamic_slice_in_dim(attention, shard_idx * out_rows, out_rows, axis=1)
        partial_out = jnp.dot(attn_mine, w_out, preferred_element_type=jnp.float32)
        attn_out = lax.psum(partial_out, 'sp').astype(jnp.bfloat16)
        return attn_out, k_next, v_next

    return jax.shard_map(local_step, mesh=mesh, in_specs=(row_spec, P(), P(), P(), P('sp', None), cache_spec, cache_spec, len_spec, len_spec), out_specs=(row_spec, cache_spec, cache_spec), check_vma=False)
```

profile of v0, /device:TPU:97, one launch (start us, length us, event | category | flops | bytes accessed | tf_op | source)
XLA Modules:
  0.0 201.1 jit_solution(8980458703248464823)
XLA Ops:
  7.2 0.0 copy-start
  7.2 0.1 all-reduce.3.cloned.1.call-start
  7.3 1.5 copy-done
  8.8 1.5 convolution_convert_fusion.2
  10.3 0.0 slice-start
  10.3 2.4 %convolution_convert_fusion.1 = bf16[64,256]{1,0:T(8,128)(2,1)S(1)} fusion(bf16[64,4096]{1,0:T(8,128)(2,1)} %param.9, bf16[4096,256]{1,0:T(8,128)(2,1)} %param.12), kind=kOutput, calls=%fused_computation.12 | convolution fusion | flops 134234112 | bytes 2654208 | tf_op jit(solution)/shard_map/dot_general | solution.py:22
  12.7 0.0 copy-start.4
  12.7 0.0 copy-start.5
  12.7 0.0 slice-start.1
  12.7 16.8 %convolution_convert_fusion = bf16[64,4096]{1,0:T(8,128)(2,1)S(1)} fusion(bf16[64,4096]{1,0:T(8,128)(2,1)} %param.9, bf16[4096,4096]{1,0:T(8,128)(2,1)} %param.10), kind=kOutput, calls=%fused_computation.6 | convolution fusion | flops 2147745792 | bytes 34603008 | tf_op jit(solution)/shard_map/dot_general | solution.py:19
  29.5 0.1 copy.24
  29.6 0.0 copy-done.4
  29.6 0.0 copy-done.5
  29.6 0.1 broadcast_compare_fusion.1
  29.7 0.0 slice-done
  29.7 0.0 slice-done.1
  29.7 8.0 %broadcast_select_fusion = (bf16[64,256,1,256]{3,1,2,0:T(8,128)(2,1)}, bf16[64,256,1,256]{3,1,2,0:T(8,128)(2,1)S(1)}) fusion(bf16[64,256,1,256]{3,1,2,0:T(8,128)(2,1)S(1)} %bitcast.47, pred[64,256]{1,0:T(8,128)(4,1)S(1)} %get-tuple-element.10, bf16[64,256]{1,0:T(8,128)(2,1)S(1)} %convolution_convert_fusion.1, bf16[64,256,1,256]{3,1,2,0:T(8,128)(2,1)} %param.14, ...), kind=kLoop, calls=%fused_computation.4 | loop fusion | flops 8388608 | bytes 33636352 | tf_op jit(solution)/shard_map/jit(_where)/select_n | solution.py:26
  37.8 0.0 copy-start.2
  37.8 3.4 %copy-done.2 = bf16[64,256,1,256]{3,1,2,0:T(8,128)(2,1)} copy-done((bf16[64,256,1,256]{3,1,2,0:T(8,128)(2,1)}, bf16[64,256,1,256]{3,1,2,0:T(8,128)(2,1)S(1)}, u32[]{:S(2)}) %copy-start.2) | copy-done | bytes 8388632
  41.2 2.4 %fusion.27 = (f32[64,16]{1,0:T(8,128)S(1)}, f32[64,16,256]{2,1,0:T(8,128)S(1)}) fusion(bf16[64,16,256]{2,1,0:T(8,128)(2,1)S(1)} %bitcast.49, bf16[64,256,1,256]{3,1,2,0:T(8,128)(2,1)S(1)} %get-tuple-element.8, pred[64,256]{1,0:T(8,128)(4,1)S(1)} %get-tuple-element.9), kind=kOutput, calls=%fused_computation.32 | convolution fusion | flops 135003136 | bytes 9981952 | tf_op jit(solution)/shard_map/bkgd,bskd->bkgs/dot_general | solution.py:27
  43.5 24.0 %pmax.7 = f32[64,1,16]{2,0,1:T(8,128)S(1)} all-reduce(f32[64,1,16]{2,0,1:T(8,128)S(1)} %get-tuple-element.5), channel_id=1, replica_groups=mesh['rep'=1,'dp'=4,'sp'=8] {'sp'}, use_global_device_ids=true, to_apply=%region_1.2 | all-reduce | flops 1024 | bytes 8192 | tf_op jit(solution)/shard_map/pmax | solution.py:34
  67.6 0.4 fusion.17
  68.0 1.2 copy.18
  69.2 0.0 copy-start.3
  69.2 0.0 copy-start.1
  69.2 4.8 %fusion.10 = f32[64,1,16,256]{3,2,0,1:T(8,128)S(1)} fusion(bf16[64,256,1,256]{3,1,2,0:T(8,128)(2,1)} %get-tuple-element.7, f32[64,16,256]{2,1,0:T(8,128)S(1)} %get-tuple-element.12, f32[64,16]{1,0:T(8,128)S(1)} %get-tuple-element.3, f32[64,16]{1,0:T(8,128)S(1)} %get-tuple-element.6), kind=kOutput, calls=%fused_computation.10 | convolution fusion | flops 135004160 | bytes 10493952 | tf_op jit(solution)/shard_map/bkgs,bskd->bkgd/dot_general | solution.py:33
  74.0 0.0 copy-done.3
  74.0 1.3 pad_maximum_fusion
  75.3 0.1 all-reduce.3.cloned.1.call-update
  75.4 60.3 %all-reduce.3.cloned.1.call-done = f32[64,1,16,257]{3,2,0,1:T(8,128)} async-done(((f32[64,1,16,257]{3,2,0,1:T(8,128)}), f32[64,1,16,257]{3,2,0,1:T(8,128)}) %all-reduce.3.cloned.1.call-update) | async-done | bytes 1052688 | tf_op jit(solution)/shard_map/psum | solution.py:37
  135.7 1.1 slice.9
  136.8 0.4 copy.23
  137.2 1.4 fusion.16
  138.7 0.2 copy.25
  138.9 3.0 %fusion.21 = f32[64,4096]{1,0:T(8,128)S(1)} fusion(bf16[512,4096]{1,0:T(8,128)(2,1)} %param.13, bf16[64,4096]{1,0:T(8,128)(2,1)S(1)} %bitcast.51, s32[]{:T(128)S(6)} %select_n.18), kind=kOutput, calls=%fused_computation.20 | convolution fusion | flops 268435456 | bytes 5308420 | tf_op jit(solution)/shard_map/dot_general | solution.py:42
  141.9 52.3 %all-reduce.4 = bf16[64,4096]{1,0:T(8,128)(2,1)} all-reduce(f32[64,4096]{1,0:T(8,128)S(1)} %fusion.21), channel_id=1, replica_groups=mesh['rep'=1,'dp'=4,'sp'=8] {'sp'}, use_global_device_ids=true, to_apply=%region_4.5 | all-reduce | flops 262144 | bytes 1572864 | tf_op jit(solution)/shard_map/psum | solution.py:43
  194.2 0.0 copy-done.1
  (4 shorter events, 0.0 us)
Async XLA Ops:
  7.2 1.6 copy-start
  7.2 128.5 %all-reduce.3.cloned.1.call-start = ((), (), s32[]{:S(2)}) async-start(), calls=%async_computation | async-start | bytes 3145728 | tf_op jit(solution)/shard_map/psum | solution.py:37
  10.3 19.4 %slice-start = ((s8[8388608]{0:T(1024)(128)(4,1)}), s8[4194304]{0:T(1024)(128)(4,1)S(1)}, s32[]{:S(2)}) async-start(s8[8388608]{0:T(1024)(128)(4,1)} %bitcast.46), calls=%async_computation.1 | async-start | bytes 8388608
  12.7 16.9 %copy-start.4 = (s32[64]{0:T(128)S(1)}, s32[64]{0:T(128)}, u32[]{:S(2)}) copy-start(s32[64]{0:T(128)} %param.17) | copy-start | bytes 772
  12.7 16.9 %copy-start.5 = (s32[64]{0:T(128)S(1)}, s32[64]{0:T(128)}, u32[]{:S(2)}) copy-start(s32[64]{0:T(128)} %param.16) | copy-start | bytes 772
  12.7 17.0 %slice-start.1 = ((s8[8388608]{0:T(1024)(128)(4,1)}), s8[4194304]{0:T(1024)(128)(4,1)S(1)}, s32[]{:S(2)}) async-start(s8[8388608]{0:T(1024)(128)(4,1)} %bitcast.46), calls=%async_computation.2 | async-start | bytes 8388608
  37.8 3.4 %copy-start.2 = (bf16[64,256,1,256]{3,1,2,0:T(8,128)(2,1)}, bf16[64,256,1,256]{3,1,2,0:T(8,128)(2,1)S(1)}, u32[]{:S(2)}) copy-start(bf16[64,256,1,256]{3,1,2,0:T(8,128)(2,1)S(1)} %get-tuple-element.8) | copy-start | bytes 25165828
  69.2 4.8 %copy-start.3 = (f32[64,1,16,1]{3,2,0,1:T(8,128)S(1)}, f32[64,1,16,1]{3,2,0,1:T(8,128)}, u32[]{:S(2)}) copy-start(f32[64,1,16,1]{3,2,0,1:T(8,128)} %copy.18) | copy-start | bytes 12292
  69.2 125.0 %copy-start.1 = (bf16[4096,256]{1,0:T(8,128)(2,1)S(1)}, bf16[4096,256]{1,0:T(8,128)(2,1)}, u32[]{:S(2)}) copy-start(bf16[4096,256]{1,0:T(8,128)(2,1)} %param.11) | copy-start | bytes 6291460
Sparse Core Ops, SparseCore 0:
  75.5 60.1 all-reduce.2
where the time goes:
time: 202 us; the launch traced here: 201 us
  blocking collectives  76.4 us (38%)
  waiting for transfers between devices  60.4 us (30%)
  matrix products  30.9 us (15%)
  between operations  14.2 us (7%)
  other arithmetic  11.2 us (6%)
  local copies, waits for them, and re-layouts  7.97 us (4%)
    psum x1, waiting for transfers between devices, local_step(): packed = lax.psum(packed, 'sp')  60.3 us
    psum x1, blocking collectives, local_step(): attn_out = lax.psum(partial_out, 'sp').astype(jnp.bfloat16)  52.3 us
    pmax x1, blocking collectives, local_step(): global_max = lax.pmax(local_max, 'sp')  24 us
    dot_general x1, matrix products, local_step(): jnp.dot(hidden, w_query, preferred_element_type=jnp.float32)  16.8 us
    select_n x1, other arithmetic, local_step(): jnp.where(at_pos, value_new.reshape(num_rows, 1, kv_heads, head_dim), v_c...  8.02 us
    unnamed x18, local copies, waits for them, and re-layouts  5.22 us
    dot_general x1, matrix products, local_step(): jnp.einsum('bkgs,bskd->bkgd', weights.astype(jnp.bfloat16), v_next, prefe...  4.82 us
  transfers between devices with their start and end apart: 1, of which 1 were waited for; matrix products, arithmetic and copies ran while one was open for 0% of the time, Pallas kernels for 0%

commit v1 on v0

v1 whole, which is shorter than its diff:
```python
import functools

import jax
import jax.numpy as jnp
from jax import lax
from jax.experimental import pallas as pl
from jax.experimental.pallas import tpu as pltpu
from jax.sharding import PartitionSpec as P

MESH = pl.DeviceIdType.MESH
NEG = -3.4e38
LANES = 128
F32 = jnp.float32
BF16 = jnp.bfloat16


def sp_dev(i):
    return {'sp': i}


def enter(n):
    me = lax.axis_index('sp')
    bar = pltpu.get_barrier_semaphore()
    for d in range(1, n):
        pl.semaphore_signal(bar, inc=1, device_id=sp_dev(lax.rem(me + d, n)), device_id_type=MESH)
    pl.semaphore_wait(bar, n - 1)


def rcopy(src, dst, ss, rs, dev):
    return pltpu.make_async_remote_copy(src_ref=src, dst_ref=dst, send_sem=ss, recv_sem=rs,
                                        device_id=sp_dev(dev), device_id_type=MESH)


def qkv_kernel(n, hid_hbm, wq_hbm, wk_hbm, wv_hbm, q_ref, kn_ref, vn_ref,
               hid, wq, wkv, hsem, wsem, ssem, rsem, psend, precv):
    nx = n // 2
    me = lax.axis_index('sp')
    x, c = me // 2, lax.rem(me, 2)
    cols = wq.shape[2]
    own = me
    opp = 2 * lax.rem(x + nx // 2, nx) + c
    partner = 2 * x + 1 - c
    ch = pltpu.make_async_copy(hid_hbm, hid, hsem)
    ch.start()
    blocks = (own, opp)
    loads = []
    for i, blk in enumerate(blocks):
        cp = pltpu.make_async_copy(wq_hbm.at[:, pl.ds(pl.multiple_of(blk * cols, cols), cols)], wq.at[i], wsem.at[i])
        cp.start()
        loads.append(cp)
    for i, w in enumerate((wk_hbm, wv_hbm)):
        cp = pltpu.make_async_copy(w, wkv.at[i], wsem.at[2 + i])
        cp.start()
        loads.append(cp)
    enter(n)
    ch.wait()

    def project(w):
        return jnp.dot(hid[...], w, preferred_element_type=F32).astype(BF16)

    loads[0].wait()
    q_ref[own] = project(wq[0])
    sends = [rcopy(q_ref.at[own], q_ref.at[own], psend.at[0], precv.at[0], partner)]
    for d in range(2):
        nb = lax.rem(x + (1 if d == 0 else nx - 1), nx)
        for t in range(2):
            sends.append(rcopy(q_ref.at[own], q_ref.at[own], ssem.at[d, t], rsem.at[d, c], 2 * nb + t))
    for s in sends[1:]:
        s.start()
    sends[0].start()
    loads[1].wait()
    q_ref[opp] = project(wq[1])
    po = rcopy(q_ref.at[opp], q_ref.at[opp], psend.at[1], precv.at[1], partner)
    po.start()
    sends.append(po)
    loads[2].wait()
    kn_ref[...] = project(wkv[0]).astype(F32)
    loads[3].wait()
    vn_ref[...] = project(wkv[1]).astype(F32)
    for s in sends:
        s.wait_send()
    pown, popp = partner, 2 * lax.rem(x + nx // 2, nx) + 1 - c
    rcopy(q_ref.at[own], q_ref.at[pown], psend.at[0], precv.at[0], partner).wait_recv()
    rcopy(q_ref.at[own], q_ref.at[popp], psend.at[1], precv.at[1], partner).wait_recv()
    for d in range(2):
        src = lax.rem(x + (nx - 1 if d == 0 else 1), nx)
        for t in range(2):
            rcopy(q_ref.at[own], q_ref.at[2 * src + t], ssem.at[d, t], rsem.at[d, t], partner).wait_recv()


def attn_kernel(group, scale, wp, vl, q_ref, kn_ref, vn_ref, k_hbm, v_hbm, ko_hbm, vo_hbm, acc_ref, ml_ref,
                kb, vb, qs, lsem, osem):
    rows, seq, hd = kb.shape
    heads = acc_ref.shape[1] // rows
    halves = hd // LANES
    steps = rows // group
    base = lax.axis_index('sp') * seq

    def load(g, start=True):
        s = pl.ds(g * group, group)
        return (pltpu.make_async_copy(k_hbm.at[s], kb.at[s], lsem.at[0, g]),
                pltpu.make_async_copy(v_hbm.at[s], vb.at[s], lsem.at[1, g]))

    def store(g):
        s = pl.ds(g * group, group)
        return (pltpu.make_async_copy(kb.at[s], ko_hbm.at[s], osem.at[0, g]),
                pltpu.make_async_copy(vb.at[s], vo_hbm.at[s], osem.at[1, g]))

    for g in range(steps):
        for cp in load(g):
            cp.start()
    per = q_ref.shape[2] // hd
    for h in range(heads):
        for z in range(halves):
            lo = (h % per) * hd + z * LANES
            qs[z, h * rows:(h + 1) * rows, :] = q_ref[h // per, :, lo:lo + LANES].astype(F32)

    pos_iota = lax.broadcasted_iota(jnp.int32, (heads, seq), 1)
    row_iota = lax.broadcasted_iota(jnp.int32, (16, hd), 0)
    lane_iota = lax.broadcasted_iota(jnp.int32, (heads, 128), 1)

    def put(buf, new, b, pos):
        start = pl.multiple_of((jnp.clip(pos, 0, seq - 1) // 16) * 16, 16)
        slab = buf[b, pl.ds(start, 16), :].astype(F32)
        row = jnp.broadcast_to(new[pl.ds(b, 1), :], slab.shape)
        buf[b, pl.ds(start, 16), :] = jnp.where(row_iota == pos - start, row, slab).astype(BF16)

    def step(g, carry):
        m_all, l_all = carry
        for cp in load(g):
            cp.wait()
        b0 = g * group
        for r in range(group):
            pos = wp[b0 + r] - base
            put(kb, kn_ref, b0 + r, pos)
            put(vb, vn_ref, b0 + r, pos)
        for cp in store(g):
            cp.start()
        scores = []
        for r in range(group):
            qb = jnp.concatenate([qs[z, pl.ds(b0 + r, heads, stride=rows), :] for z in range(halves)], axis=1).astype(BF16)
            scores.append(lax.dot_general(qb, kb[b0 + r], (((1,), (1,)), ((), ())), preferred_element_type=F32))
        probs = []
        for r in range(group):
            valid = pos_iota < vl[b0 + r] - base
            s = jnp.where(valid, scores[r] * scale, NEG)
            m = jnp.max(s, axis=1, keepdims=True)
            p = jnp.where(valid, jnp.exp(s - m), 0.0)
            l = jnp.sum(p, axis=1, keepdims=True)
            here = lane_iota == b0 + r
            m_all = jnp.where(here, m, m_all)
            l_all = jnp.where(here, l, l_all)
            probs.append(p.astype(BF16))
        for r in range(group):
            o = jnp.dot(probs[r], vb[b0 + r], preferred_element_type=F32)
            for z in range(halves):
                acc_ref[z, pl.ds(b0 + r, heads, stride=rows), :] = o[:, z * LANES:(z + 1) * LANES]
        return m_all, l_all

    m_all, l_all = lax.fori_loop(0, steps, step, (jnp.full((heads, 128), NEG, F32), jnp.zeros((heads, 128), F32)))
    for i in range(ml_ref.shape[0]):
        ml_ref[i, 0:per, :] = m_all[i * per:(i + 1) * per]
        ml_ref[i, per:2 * per, :] = l_all[i * per:(i + 1) * per]
    for g in range(steps):
        for cp in store(g):
            cp.wait()


def out_kernel(n, acc_ref, ml_ref, w_hbm, out_ref, wv, ra, rml, sb, sml, rb, rbml, sd, rd, se, re,
               wsem, asend, arecv, amsend, amrecv, bsend, brecv, bmsend, bmrecv, dsend, drecv, esend, erecv,
               fsend, frecv, gsend, grecv):
    nx = n // 2
    me = lax.axis_index('sp')
    x, c = me // 2, lax.rem(me, 2)
    partner = 2 * x + 1 - c
    wide = wv.shape[2]
    blk_rows = ra.shape[2]
    halves = acc_ref.shape[0]
    rows = out_ref.shape[0]
    per = blk_rows // rows
    order = [2, 1, 3, 0] if nx == 4 else list(range(1, nx)) + [0]

    wloads = []
    for j in range(n):
        cp = pltpu.make_async_copy(w_hbm.at[:, j * wide:(j + 1) * wide], wv.at[j], wsem.at[j])
        cp.start()
        wloads.append(cp)
    enter(n)

    def chip(d):
        return lax.rem(x + d, nx)

    def acc_at(j):
        return acc_ref.at[:, pl.ds(pl.multiple_of(j * blk_rows, blk_rows), blk_rows)]

    pending = []
    for d in order:
        j = 2 * chip(d) + 1 - c
        a = rcopy(acc_at(j), ra.at[d], asend.at[d], arecv.at[d], partner)
        b = rcopy(ml_ref.at[j], rml.at[d], amsend.at[d], amrecv.at[d], partner)
        b.start()
        a.start()
        pending += [a, b]
    for d in order:
        j = 2 * chip(d) + c
        rcopy(acc_at(j), ra.at[d], asend.at[d], arecv.at[d], partner).wait_recv()
        rcopy(ml_ref.at[j], rml.at[d], amsend.at[d], amrecv.at[d], partner).wait_recv()
        mine, theirs = ml_ref[j], rml[d]
        m = jnp.maximum(mine[0:per], theirs[0:per])
        ca, cb = jnp.exp(mine[0:per] - m), jnp.exp(theirs[0:per] - m)
        l = ca * mine[per:2 * per] + cb * theirs[per:2 * per]
        cols = jnp.transpose(jnp.concatenate([ca, cb, m, l], axis=0))
        sml[d, 0:per, :] = m
        sml[d, per:2 * per, :] = l
        for h in range(per):
            r = slice(h * rows, (h + 1) * rows)
            for z in range(halves):
                own = acc_ref[z, pl.ds(pl.multiple_of(j * blk_rows + h * rows, rows), rows), :]
                sb[d, z, r, :] = own * cols[0:rows, h:h + 1] + ra[d, z, r, :] * cols[0:rows, per + h:per + h + 1]
        if d:
            a = rcopy(sb.at[d], rb.at[d], bsend.at[d], brecv.at[d], j)
            b = rcopy(sml.at[d], rbml.at[d], bmsend.at[d], bmrecv.at[d], j)
            b.start()
            a.start()
            pending += [a, b]
    for d in range(1, nx):
        rcopy(sb.at[d], rb.at[d], bsend.at[d], brecv.at[d], me ^ 1).wait_recv()
        rcopy(sml.at[d], rbml.at[d], bmsend.at[d], bmrecv.at[d], me ^ 1).wait_recv()
    mls = [sml[0]] + [rbml[d] for d in range(1, nx)]
    m = functools.reduce(jnp.maximum, [t[0:per] for t in mls])
    cs = [jnp.exp(t[0:per] - m) for t in mls]
    l = sum(cf * t[per:2 * per] for cf, t in zip(cs, mls))
    cols = jnp.transpose(jnp.concatenate([cf / l for cf in cs], axis=0))
    heads = []
    for h in range(per):
        r = slice(h * rows, (h + 1) * rows)
        for z in range(halves):
            parts = [sb[0, z, r, :]] + [rb[d, z, r, :] for d in range(1, nx)]
            heads.append(sum(part * cols[0:rows, d * per + h:d * per + h + 1] for d, part in enumerate(parts)))
    attn = jnp.concatenate(heads, axis=1).astype(BF16)

    for cp in wloads:
        cp.wait()
    for d in order:
        sd[d] = jnp.dot(attn, wv[2 * chip(d) + 1 - c], preferred_element_type=F32)
        a = rcopy(sd.at[d], rd.at[d], dsend.at[d], drecv.at[d], partner)
        a.start()
        pending.append(a)
    for d in order:
        j = 2 * chip(d) + c
        part = jnp.dot(attn, wv[j], preferred_element_type=F32)
        rcopy(sd.at[d], rd.at[d], dsend.at[d], drecv.at[d], partner).wait_recv()
        se[d] = part + rd[d]
        if d:
            a = rcopy(se.at[d], re.at[d], esend.at[d], erecv.at[d], j)
            a.start()
            pending.append(a)
    for d in range(1, nx):
        rcopy(se.at[d], re.at[d], esend.at[d], erecv.at[d], partner).wait_recv()

    def out_at(j):
        return out_ref.at[:, pl.ds(pl.multiple_of(j * wide, wide), wide)]

    out_ref[:, pl.ds(pl.multiple_of(me * wide, wide), wide)] = (
        se[0] + sum(re[d] for d in range(1, nx))).astype(BF16)
    for d in order[:-1]:
        a = rcopy(out_at(me), out_at(me), fsend.at[d], frecv.at[d], 2 * chip(d) + c)
        a.start()
        pending.append(a)
    a = rcopy(out_at(me), out_at(me), gsend.at[0], grecv.at[0], partner)
    a.start()
    pending.append(a)
    near = order[1:-1] + order[:1]
    for d in near:
        src = 2 * chip(nx - d) + c
        rcopy(out_at(me), out_at(src), fsend.at[d], frecv.at[d], partner).wait_recv()
        a = rcopy(out_at(src), out_at(src), gsend.at[d], grecv.at[d], partner)
        a.start()
        pending.append(a)
    for d in [0] + near:
        src = 2 * chip(nx - d if d else 0) + 1 - c
        rcopy(out_at(me), out_at(src), gsend.at[d], grecv.at[d], partner).wait_recv()
    for a in pending:
        a.wait_send()


def solution(mesh):
    n = mesh.shape['sp']
    nx = n // 2
    row_spec = P(('rep', 'dp'), None)
    cache_spec = P(('rep', 'dp'), 'sp', None, None)
    len_spec = P(('rep', 'dp'))
    VM = pl.BlockSpec(memory_space=pltpu.VMEM)
    HB = pl.BlockSpec(memory_space=pltpu.HBM)
    SM = pl.BlockSpec(memory_space=pltpu.SMEM)
    DMA = pltpu.SemaphoreType.DMA

    def local_step(hidden, w_query, w_key, w_value, w_out, k_cache, v_cache, write_pos, valid_len):
        rows, seq, kv_heads, hd = k_cache.shape
        width = hidden.shape[1]
        proj = w_query.shape[1]
        heads = proj // hd
        cols = proj // n
        per = heads // n
        k3, v3 = k_cache.reshape(rows, seq, hd), v_cache.reshape(rows, seq, hd)
        sds = jax.ShapeDtypeStruct

        q, kn, vn = pl.pallas_call(
            functools.partial(qkv_kernel, n),
            out_shape=(sds((n, rows, cols), BF16), sds((rows, hd), F32), sds((rows, hd), F32)),
            in_specs=[HB] * 4, out_specs=(VM, VM, VM),
            scratch_shapes=[pltpu.VMEM((rows, width), BF16), pltpu.VMEM((2, width, cols), BF16),
                            pltpu.VMEM((2, width, hd), BF16), DMA, DMA((4,)), DMA((2, 2)), DMA((2, 2)),
                            DMA((2,)), DMA((2,))],
            compiler_params=pltpu.CompilerParams(collective_id=0, has_side_effects=True,
                                                 vmem_limit_bytes=32 * 2 ** 20),
            name='qkv',
        )(hidden, w_query, w_key, w_value)

        group = 8
        k_new, v_new, acc, ml = pl.pallas_call(
            functools.partial(attn_kernel, group, hd ** -0.5),
            out_shape=(sds((rows, seq, hd), BF16), sds((rows, seq, hd), BF16), sds((hd // LANES, heads * rows, LANES), F32),
                       sds((n, 8, 128), F32)),
            in_specs=[SM, SM, VM, VM, VM, HB, HB], out_specs=(HB, HB, VM, VM),
            scratch_shapes=[pltpu.VMEM((rows, seq, hd), BF16), pltpu.VMEM((rows, seq, hd), BF16),
                            pltpu.VMEM((hd // LANES, heads * rows, LANES), F32), DMA((2, rows // group)), DMA((2, rows // group))],
            compiler_params=pltpu.CompilerParams(vmem_limit_bytes=40 * 2 ** 20),
            name='attn',
        )(write_pos, valid_len, q, kn, vn, k3, v3)

        blk = per * rows
        wide = width // n
        f = pltpu.VMEM
        out = pl.pallas_call(
            functools.partial(out_kernel, n),
            out_shape=sds((rows, width), BF16),
            in_specs=[VM, VM, HB], out_specs=VM,
            scratch_shapes=[f((n, w_out.shape[0], wide), BF16),
                            f((nx, hd // LANES, blk, LANES), F32), f((nx, 8, 128), F32), f((nx, hd // LANES, blk, LANES), F32), f((nx, 8, 128), F32),
                            f((nx, hd // LANES, blk, LANES), F32), f((nx, 8, 128), F32),
                            f((nx, rows, wide), F32), f((nx, rows, wide), F32),
                            f((nx, rows, wide), F32), f((nx, rows, wide), F32),
                            DMA((n,))] + [DMA((nx,))] * 16,
            compiler_params=pltpu.CompilerParams(collective_id=1, has_side_effects=True,
                                                 vmem_limit_bytes=32 * 2 ** 20),
            name='outp',
        )(acc, ml, w_out)
        return out, k_new.reshape(k_cache.shape), v_new.reshape(v_cache.shape)

    return jax.shard_map(local_step, mesh=mesh,
                         in_specs=(row_spec, P(), P(), P(), P('sp', None), cache_spec, cache_spec, len_spec, len_spec),
                         out_specs=(row_spec, cache_spec, cache_spec), check_vma=False)
```

time: 202 us -> 55.5 us (0.27)
  blocking collectives: 76.4 us -> 0 us
  waiting for transfers between devices: 60.4 us -> 0 us
  Pallas kernels: 0 us -> 49.6 us
  matrix products: 30.9 us -> 0 us
  between operations: 14.2 us -> 0.71 us
  other arithmetic: 11.2 us -> 0 us
  local copies, waits for them, and re-layouts: 7.97 us -> 5.03 us
    psum x1 -> x0, waiting for transfers between devices: 60.3 us -> none  [local_step(): packed = lax.psum(packed, 'sp')]
    psum x1 -> x0, blocking collectives: 52.3 us -> none  [local_step(): attn_out = lax.psum(partial_out, 'sp').astype(jnp.bfloat16)]
    pallas_call x0 -> x3, Pallas kernels: none -> 49.6 us  [the longest x1 29.4 us: local_step(): pl.pallas_call(functools.partial(out_kernel, n), out_shape=sds((rows, wid...]
    dot_general x6 -> x0, matrix products: 30.9 us -> none  [the longest x1 16.8 us: local_step(): jnp.dot(hidden, w_query, preferred_element_type=jnp.float32)]
    pmax x1 -> x0, blocking collectives: 24 us -> none  [local_step(): global_max = lax.pmax(local_max, 'sp')]
    select_n x1 -> x0, other arithmetic: 8.02 us -> none  [local_step(): jnp.where(at_pos, value_new.reshape(num_rows, 1, kv_heads, head_dim), v_c...]
    unnamed x18 -> x15, local copies, waits for them, and re-layouts: 5.22 us -> 5.03 us
  transfers between devices with their start and end apart: 1 -> 0, of which waited for: 1 -> 0; matrix products, arithmetic and copies ran while one was open for 0% -> 0% of each run, Pallas kernels for 0% -> 0%
where the time goes in v1:
time: 55.5 us; the launch traced here: 55.3 us
  Pallas kernels  49.6 us (89%)
  local copies, waits for them, and re-layouts  5.03 us (9%)
  between operations  0.71 us (1%)
    pallas_call x1, Pallas kernels, local_step(): pl.pallas_call(functools.partial(out_kernel, n), out_shape=sds((rows, wid...  29.4 us
    pallas_call x1, Pallas kernels, local_step(): pl.pallas_call(functools.partial(qkv_kernel, n), out_shape=(sds((n, rows,...  10.8 us
    pallas_call x1, Pallas kernels, local_step(): pl.pallas_call(functools.partial(attn_kernel, group, hd ** (-0.5)), out_s...  9.41 us
    unnamed x15, local copies, waits for them, and re-layouts  5.03 us

profile of v1, /device:TPU:97, one launch (start us, length us, event | category | flops | bytes accessed | tf_op | source)
XLA Modules:
  0.0 55.3 jit_solution(8468176079229664933)
XLA Ops:
  0.6 0.0 copy-start.2
  0.6 1.6 %copy-done.2 = bf16[4096,256]{1,0:T(8,128)(2,1)S(1)} copy-done((bf16[4096,256]{1,0:T(8,128)(2,1)S(1)}, bf16[4096,256]{1,0:T(8,128)(2,1)}, u32[]{:S(2)}) %copy-start.2) | copy-done | bytes 2097176
  2.2 0.0 copy-start.3
  2.2 1.6 %copy-done.3 = bf16[4096,256]{1,0:T(8,128)(2,1)S(1)} copy-done((bf16[4096,256]{1,0:T(8,128)(2,1)S(1)}, bf16[4096,256]{1,0:T(8,128)(2,1)}, u32[]{:S(2)}) %copy-start.3) | copy-done | bytes 2097176
  3.8 0.0 copy-start.4
  3.8 1.0 %copy-done.4 = bf16[64,4096]{1,0:T(8,128)(2,1)S(1)} copy-done((bf16[64,4096]{1,0:T(8,128)(2,1)S(1)}, bf16[64,4096]{1,0:T(8,128)(2,1)}, u32[]{:S(2)}) %copy-start.4) | copy-done | bytes 524312
  4.9 0.0 copy-start
  4.9 0.0 copy-start.5
  4.9 0.0 copy-start.6
  4.9 10.8 %qkv.1 = (bf16[8,64,512]{2,1,0:T(8,128)(2,1)S(1)}, f32[64,256]{1,0:T(8,128)S(1)}, f32[64,256]{1,0:T(8,128)S(1)}) custom-call(bf16[64,4096]{1,0:T(8,128)(2,1)S(1)} %copy-done.4, bf16[4096,4096]{1,0:T(8,128)(2,1)} %wq_hbm.1, bf16[4096,256]{1,0:T(8,128)(2,1)S(1)} %copy-done.2, bf16[4096,256]{1,0:T(8,128)(2,1)S(1)} %copy-done.3), custom_call_target="tpu_custom_call" | custom-call | tf_op jit(solution)/shard_map/qkv/pallas_call | solution.py:308
  15.7 0.0 copy-done
  15.7 0.0 copy-done.5
  15.7 0.0 copy-done.6
  15.7 0.0 copy-start.1
  15.8 9.4 %attn.1 = (bf16[64,256,256]{2,1,0:T(8,128)(2,1)}, bf16[64,256,256]{2,1,0:T(8,128)(2,1)}, f32[2,1024,128]{2,1,0:T(8,128)S(1)}, f32[8,8,128]{2,1,0:T(8,128)S(1)}) custom-call(s32[64]{0:T(128)S(1)} %copy-done.5, s32[64]{0:T(128)S(1)} %copy-done.6, bf16[8,64,512]{2,1,0:T(8,128)(2,1)S(1)} %get-tuple-element.10.q_ref, f32[64,256]{1,0:T(8,128)S(1)} %get-tuple-element.11.kn_ref, ...), custom_call_target="tpu_custom_call" | custom-call | tf_op jit(solution)/shard_map/attn/pallas_call | solution.py:321
  25.2 0.0 copy-done.1
  25.2 29.4 %outp.1 = bf16[64,4096]{1,0:T(8,128)(2,1)S(1)} custom-call(f32[2,1024,128]{2,1,0:T(8,128)S(1)} %get-tuple-element.13.acc_ref, f32[8,8,128]{2,1,0:T(8,128)S(1)} %get-tuple-element.14.ml_ref, bf16[512,4096]{1,0:T(8,128)(2,1)S(1)} %copy-done.1), custom_call_target="tpu_custom_call" | custom-call | tf_op jit(solution)/shard_map/outp/pallas_call | solution.py:335
  54.5 0.8 %copy.15 = bf16[64,4096]{1,0:T(8,128)(2,1)} copy(bf16[64,4096]{1,0:T(8,128)(2,1)S(1)} %outp.1) | data formatting | bytes 1048576
Async XLA Ops:
  0.6 1.6 %copy-start.2 = (bf16[4096,256]{1,0:T(8,128)(2,1)S(1)}, bf16[4096,256]{1,0:T(8,128)(2,1)}, u32[]{:S(2)}) copy-start(bf16[4096,256]{1,0:T(8,128)(2,1)} %wk_hbm.1) | copy-start | bytes 6291460
  2.2 1.6 %copy-start.3 = (bf16[4096,256]{1,0:T(8,128)(2,1)S(1)}, bf16[4096,256]{1,0:T(8,128)(2,1)}, u32[]{:S(2)}) copy-start(bf16[4096,256]{1,0:T(8,128)(2,1)} %wv_hbm.1) | copy-start | bytes 6291460
  3.8 1.0 %copy-start.4 = (bf16[64,4096]{1,0:T(8,128)(2,1)S(1)}, bf16[64,4096]{1,0:T(8,128)(2,1)}, u32[]{:S(2)}) copy-start(bf16[64,4096]{1,0:T(8,128)(2,1)} %hid_hbm.1) | copy-start | bytes 1572868
  4.9 10.9 %copy-start = (bf16[64,256,1,256]{3,1,2,0:T(8,128)(2,1)S(1)}, bf16[64,256,1,256]{3,1,2,0:T(8,128)(2,1)}, u32[]{:S(2)}) copy-start(bf16[64,256,1,256]{3,1,2,0:T(8,128)(2,1)} %param.14) | copy-start | bytes 25165828
  4.9 10.9 %copy-start.5 = (s32[64]{0:T(128)S(1)}, s32[64]{0:T(128)}, u32[]{:S(2)}) copy-start(s32[64]{0:T(128)} %wp.1) | copy-start | bytes 772
  4.9 10.9 %copy-start.6 = (s32[64]{0:T(128)S(1)}, s32[64]{0:T(128)}, u32[]{:S(2)}) copy-start(s32[64]{0:T(128)} %vl.1) | copy-start | bytes 772
  15.7 9.4 %copy-start.1 = (bf16[512,4096]{1,0:T(8,128)(2,1)S(1)}, bf16[512,4096]{1,0:T(8,128)(2,1)}, u32[]{:S(2)}) copy-start(bf16[512,4096]{1,0:T(8,128)(2,1)} %w_hbm.1) | copy-start | bytes 12582916

commit v2 on v0

v2 whole, which is shorter than its diff:
```python
import functools

import jax
import jax.numpy as jnp
from jax import lax
from jax.experimental import pallas as pl
from jax.experimental.pallas import tpu as pltpu
from jax.sharding import PartitionSpec as P

MESH = pl.DeviceIdType.MESH
NEG = -3.4e38
LANES = 128
F32 = jnp.float32
BF16 = jnp.bfloat16


def sp_dev(i):
    return {'sp': i}


def rcopy(src, dst, ss, rs, dev):
    return pltpu.make_async_remote_copy(src_ref=src, dst_ref=dst, send_sem=ss, recv_sem=rs,
                                        device_id=sp_dev(dev), device_id_type=MESH)


def qkv_kernel(n, hid_hbm, wq_hbm, wk_hbm, wv_hbm, k_hbm, v_hbm, q_ref, kv_ref, kb, vb,
               hid, wq, wkv, hsem, wsem, csem, ssem, rsem, psend, precv):
    nx = n // 2
    me = lax.axis_index('sp')
    x, c = me // 2, lax.rem(me, 2)
    cols = wq.shape[2]
    own = me
    opp = 2 * lax.rem(x + nx // 2, nx) + c
    partner = 2 * x + 1 - c
    ch = pltpu.make_async_copy(hid_hbm, hid, hsem)
    ch.start()
    loads = []
    for i, blk in enumerate((own, opp)):
        cp = pltpu.make_async_copy(wq_hbm.at[:, pl.ds(pl.multiple_of(blk * cols, cols), cols)], wq.at[i], wsem.at[i])
        cp.start()
        loads.append(cp)
    near = [lax.rem(x + d, nx) for d in (1, nx - 1)]
    bar = pltpu.get_barrier_semaphore()
    peers = [2 * t + u for t in near for u in range(2)] + [partner]
    for peer in peers:
        pl.semaphore_signal(bar, inc=1, device_id=sp_dev(peer), device_id_type=MESH)
    pick = [pltpu.make_async_copy(w, wkv, wsem.at[2]) for w in (wk_hbm, wv_hbm)]
    for i in range(2):
        @pl.when(c == i)
        def _():
            pick[i].start()
    ch.wait()
    loads[0].wait()
    parts = csem.shape[1]
    step = kb.shape[0] // parts
    caches = []
    for g in range(parts):
        for i, (src, dst) in enumerate(((k_hbm, kb), (v_hbm, vb))):
            cp = pltpu.make_async_copy(src.at[pl.ds(g * step, step)], dst.at[pl.ds(g * step, step)], csem.at[i, g])
            cp.start()
            caches.append(cp)

    def project(w):
        return jnp.dot(hid[...], w, preferred_element_type=F32).astype(BF16)

    q_ref[own] = project(wq[0])
    pl.semaphore_wait(bar, len(peers))
    sends = []
    for d in range(2):
        for t in range(2):
            sends.append(rcopy(q_ref.at[own], q_ref.at[own], ssem.at[d, t], rsem.at[d, c], 2 * near[d] + t))
    sends.append(rcopy(q_ref.at[own], q_ref.at[own], psend.at[0], precv.at[0], partner))
    for s in sends:
        s.start()
    loads[1].wait()
    q_ref[opp] = project(wq[1])
    sends.append(rcopy(q_ref.at[opp], q_ref.at[opp], psend.at[1], precv.at[1], partner))
    sends[-1].start()
    pick[0].wait()
    kv_ref[c] = project(wkv[...]).astype(F32)
    sends.append(rcopy(kv_ref.at[c], kv_ref.at[c], psend.at[2], precv.at[2], partner))
    sends[-1].start()
    for s in sends:
        s.wait_send()
    popp = 2 * lax.rem(x + nx // 2, nx) + 1 - c
    rcopy(q_ref.at[own], q_ref.at[partner], psend.at[0], precv.at[0], partner).wait_recv()
    rcopy(q_ref.at[own], q_ref.at[popp], psend.at[1], precv.at[1], partner).wait_recv()
    rcopy(kv_ref.at[c], kv_ref.at[1 - c], psend.at[2], precv.at[2], partner).wait_recv()
    for d in range(2):
        for t in range(2):
            rcopy(q_ref.at[own], q_ref.at[2 * near[1 - d] + t], ssem.at[d, t], rsem.at[d, t], partner).wait_recv()
    for cp in caches:
        cp.wait()


def attn_kernel(group, chunk, scale, wp, vl, q_ref, kv_ref, k_in, v_in, ko_hbm, vo_hbm, kb, vb, acc_ref, ml_ref,
                qs, osem):
    del k_in, v_in
    rows, seq, hd = kb.shape
    heads = acc_ref.shape[1] // rows
    halves = hd // LANES
    steps = rows // group
    base = lax.axis_index('sp') * seq

    def store(g):
        s = pl.ds(g * group, group)
        return (pltpu.make_async_copy(kb.at[s], ko_hbm.at[s], osem.at[0, g]),
                pltpu.make_async_copy(vb.at[s], vo_hbm.at[s], osem.at[1, g]))

    per = q_ref.shape[2] // hd
    row_iota = lax.broadcasted_iota(jnp.int32, (16, hd), 0)

    def put(buf, i, b, pos):
        start = pl.multiple_of((jnp.clip(pos, 0, seq - 1) // 16) * 16, 16)
        slab = buf[b, pl.ds(start, 16), :].astype(F32)
        row = jnp.broadcast_to(kv_ref[i, pl.ds(b, 1), :], slab.shape)
        buf[b, pl.ds(start, 16), :] = jnp.where(row_iota == pos - start, row, slab).astype(BF16)

    def update(g, carry):
        for r in range(group):
            pos = wp[g * group + r] - base
            put(kb, 0, g * group + r, pos)
            put(vb, 1, g * group + r, pos)
        for cp in store(g):
            cp.start()
        return carry

    lax.fori_loop(0, steps, update, 0)
    for h in range(heads):
        for z in range(halves):
            lo = (h % per) * hd + z * LANES
            for t in range(rows // chunk):
                to = (t * heads + h) * chunk
                qs[z, to:to + chunk, :] = q_ref[h // per, t * chunk:(t + 1) * chunk, lo:lo + LANES].astype(F32)

    pos_iota = lax.broadcasted_iota(jnp.int32, (heads, seq), 1)
    lane_iota = lax.broadcasted_iota(jnp.int32, (heads, LANES), 1)

    def step(g, carry):
        m_all, l_all = carry
        b0 = g * group
        at0 = (b0 // chunk) * (heads * chunk) + lax.rem(b0, chunk)
        scores = []
        for r in range(group):
            qb = jnp.concatenate([qs[z, pl.ds(at0 + r, heads, stride=chunk), :] for z in range(halves)], axis=1)
            scores.append(lax.dot_general(qb.astype(BF16), kb[b0 + r], (((1,), (1,)), ((), ())),
                                          preferred_element_type=F32))
        probs = []
        for r in range(group):
            valid = pos_iota < vl[b0 + r] - base
            s = jnp.where(valid, scores[r] * scale, NEG)
            m = jnp.max(s, axis=1, keepdims=True)
            p = jnp.where(valid, jnp.exp(s - m), 0.0)
            l = jnp.sum(p, axis=1, keepdims=True)
            here = lane_iota == b0 + r
            m_all = jnp.where(here, m, m_all)
            l_all = jnp.where(here, l, l_all)
            probs.append(p.astype(BF16))
        for r in range(group):
            o = jnp.dot(probs[r], vb[b0 + r], preferred_element_type=F32)
            for z in range(halves):
                acc_ref[z, pl.ds(at0 + r, heads, stride=chunk), :] = o[:, z * LANES:(z + 1) * LANES]
        return m_all, l_all

    m_all, l_all = lax.fori_loop(0, steps, step, (jnp.full((heads, LANES), NEG, F32), jnp.zeros((heads, LANES), F32)))
    for i in range(ml_ref.shape[0]):
        ml_ref[i, 0:per, :] = m_all[i * per:(i + 1) * per]
        ml_ref[i, per:2 * per, :] = l_all[i * per:(i + 1) * per]
    for g in range(steps):
        for cp in store(g):
            cp.wait()


def out_kernel(n, acc_ref, ml_ref, w_ref, out_ref, ra, rml, ca, sb, sml, rb, rbml, cb, sd, rd, se, re,
               amsend, amrecv, bmsend, bmrecv, asend, arecv, bsend, brecv, dsend, drecv, esend, erecv,
               fsend, frecv, gsend, grecv):
    nx = n // 2
    me = lax.axis_index('sp')
    x, c = me // 2, lax.rem(me, 2)
    partner = 2 * x + 1 - c
    wide = out_ref.shape[1] // n
    halves = acc_ref.shape[0]
    chunks, blk = ra.shape[0], ra.shape[3]
    chunk = out_ref.shape[0] // chunks
    per = blk // chunk
    far = [2, 1, 3] if nx == 4 else list(range(1, nx))
    near = [1, 3, 2] if nx == 4 else list(range(1, nx))
    order = far + [0]

    def chip(d):
        return lax.rem(x + d, nx)

    bar = pltpu.get_barrier_semaphore()
    peers = [2 * chip(d) + c for d in range(1, nx)] + [partner]
    for peer in peers:
        pl.semaphore_signal(bar, inc=1, device_id=sp_dev(peer), device_id_type=MESH)
    pl.semaphore_wait(bar, len(peers))

    def acc_at(t, j):
        return pl.ds(pl.multiple_of((t * n + j) * blk, blk), blk)

    pending = []

    def go(*args):
        cp = rcopy(*args)
        cp.start()
        pending.append(cp)

    def landed(*args):
        rcopy(*args, partner).wait_recv()

    for d in order:
        go(ml_ref.at[2 * chip(d) + 1 - c], rml.at[d], amsend.at[d], amrecv.at[d], partner)
    for t in range(chunks):
        for d in order:
            go(acc_ref.at[:, acc_at(t, 2 * chip(d) + 1 - c)], ra.at[t, d], asend.at[t, d], arecv.at[t, d], partner)
    for d in order:
        j = 2 * chip(d) + c
        landed(ml_ref.at[j], rml.at[d], amsend.at[d], amrecv.at[d])
        mine, theirs = ml_ref[j], rml[d]
        m = jnp.maximum(mine[0:per], theirs[0:per])
        fa, fb = jnp.exp(mine[0:per] - m), jnp.exp(theirs[0:per] - m)
        l = fa * mine[per:2 * per] + fb * theirs[per:2 * per]
        ca[d] = jnp.transpose(jnp.concatenate([fa, fb, m, l], axis=0))
        sml[d, 0:per, :] = m
        sml[d, per:2 * per, :] = l
        if d:
            go(sml.at[d], rbml.at[d], bmsend.at[d], bmrecv.at[d], j)
    for t in range(chunks):
        for d in order:
            j = 2 * chip(d) + c
            landed(ra.at[t, d], ra.at[t, d], asend.at[t, d], arecv.at[t, d])
            for h in range(per):
                r = slice(h * chunk, (h + 1) * chunk)
                f = ca[d, t * chunk:(t + 1) * chunk, :]
                for z in range(halves):
                    own = acc_ref[z, pl.ds(pl.multiple_of((t * n + j) * blk + h * chunk, chunk), chunk), :]
                    sb[t, d, z, r, :] = own * f[:, h:h + 1] + ra[t, d, z, r, :] * f[:, per + h:per + h + 1]
            if d:
                go(sb.at[t, d], rb.at[t, d], bsend.at[t, d], brecv.at[t, d], j)
    for d in range(1, nx):
        landed(sml.at[d], rbml.at[d], bmsend.at[d], bmrecv.at[d])
    mls = [sml[0]] + [rbml[d] for d in range(1, nx)]
    m = functools.reduce(jnp.maximum, [u[0:per] for u in mls])
    fs = [jnp.exp(u[0:per] - m) for u in mls]
    l = sum(f * u[per:2 * per] for f, u in zip(fs, mls))
    cb[...] = jnp.transpose(jnp.concatenate([f / l for f in fs], axis=0))

    def w_at(j):
        return w_ref[:, pl.ds(pl.multiple_of(j * wide, wide), wide)]

    def out_at(t, j):
        return out_ref.at[pl.ds(t * chunk, chunk), pl.ds(pl.multiple_of(j * wide, wide), wide)]

    def project(t):
        for d in range(1, nx):
            landed(sb.at[t, d], rb.at[t, d], bsend.at[t, d], brecv.at[t, d])
        f = cb[t * chunk:(t + 1) * chunk, :]
        heads = []
        for h in range(per):
            r = slice(h * chunk, (h + 1) * chunk)
            for z in range(halves):
                terms = [sb[t, 0, z, r, :]] + [rb[t, d, z, r, :] for d in range(1, nx)]
                heads.append(sum(u * f[:, d * per + h:d * per + h + 1] for d, u in enumerate(terms)))
        attn = jnp.concatenate(heads, axis=1).astype(BF16)
        for d in order:
            sd[t, d] = jnp.dot(attn, w_at(2 * chip(d) + 1 - c), preferred_element_type=F32)
            go(sd.at[t, d], rd.at[t, d], dsend.at[t, d], drecv.at[t, d], partner)
        for d in order:
            se[t, d] = jnp.dot(attn, w_at(2 * chip(d) + c), preferred_element_type=F32)
        for d in order:
            landed(sd.at[t, d], rd.at[t, d], dsend.at[t, d], drecv.at[t, d])
            se[t, d] = se[t, d] + rd[t, d]
            if d:
                go(se.at[t, d], re.at[t, d], esend.at[t, d], erecv.at[t, d], 2 * chip(d) + c)

    def finish(t):
        for d in range(1, nx):
            landed(se.at[t, d], re.at[t, d], esend.at[t, d], erecv.at[t, d])
        out_ref[t * chunk:(t + 1) * chunk, pl.ds(pl.multiple_of(me * wide, wide), wide)] = (
            se[t, 0] + sum(re[t, d] for d in range(1, nx))).astype(BF16)
        for d in far:
            go(out_at(t, me), out_at(t, me), fsend.at[t, d], frecv.at[t, d], 2 * chip(d) + c)
        go(out_at(t, me), out_at(t, me), gsend.at[t, 0], grecv.at[t, 0], partner)

    def forward(t):
        for d in near:
            src = 2 * chip(nx - d) + c
            landed(out_at(t, me), out_at(t, src), fsend.at[t, d], frecv.at[t, d])
            go(out_at(t, src), out_at(t, src), gsend.at[t, d], grecv.at[t, d], partner)

    for t in range(chunks):
        project(t)
        if t >= 2:
            finish(t - 2)
    finish(chunks - 2)
    for t in range(chunks - 2):
        forward(t)
    finish(chunks - 1)
    forward(chunks - 2)
    forward(chunks - 1)
    for t in range(chunks):
        for d in [0] + near:
            src = 2 * chip(nx - d if d else 0) + 1 - c
            landed(out_at(t, me), out_at(t, src), gsend.at[t, d], grecv.at[t, d])
    for cp in pending:
        cp.wait_send()


def solution(mesh):
    n = mesh.shape['sp']
    nx = n // 2
    row_spec = P(('rep', 'dp'), None)
    cache_spec = P(('rep', 'dp'), 'sp', None, None)
    len_spec = P(('rep', 'dp'))
    VM = pl.BlockSpec(memory_space=pltpu.VMEM)
    HB = pl.BlockSpec(memory_space=pltpu.HBM)
    SM = pl.BlockSpec(memory_space=pltpu.SMEM)
    DMA = pltpu.SemaphoreType.DMA

    def local_step(hidden, w_query, w_key, w_value, w_out, k_cache, v_cache, write_pos, valid_len):
        rows, seq, kv_heads, hd = k_cache.shape
        width = hidden.shape[1]
        proj = w_query.shape[1]
        heads = proj // hd
        cols = proj // n
        per = heads // n
        k3, v3 = k_cache.reshape(rows, seq, hd), v_cache.reshape(rows, seq, hd)
        sds = jax.ShapeDtypeStruct

        group, chunk = 8, rows // 4
        chunks = rows // chunk
        f = pltpu.VMEM
        q, kv, kb, vb = pl.pallas_call(
            functools.partial(qkv_kernel, n),
            out_shape=(f((n, rows, cols), BF16), f((2, rows, hd), F32),
                       f((rows, seq, hd), BF16), f((rows, seq, hd), BF16)),
            in_specs=[HB] * 6, out_specs=(VM,) * 4,
            scratch_shapes=[f((rows, width), BF16), f((2, width, cols), BF16), f((width, hd), BF16),
                            DMA, DMA((3,)), DMA((2, 4)), DMA((2, 2)), DMA((2, 2)), DMA((3,)), DMA((3,))],
            compiler_params=pltpu.CompilerParams(collective_id=0, has_side_effects=True,
                                                 vmem_limit_bytes=46 * 2 ** 20),
            name='qkv',
        )(hidden, w_query, w_key, w_value, k3, v3)

        accs = f((hd // LANES, heads * rows, LANES), F32)
        k_new, v_new, _, _, acc, ml = pl.pallas_call(
            functools.partial(attn_kernel, group, chunk, hd ** -0.5),
            out_shape=(sds((rows, seq, hd), BF16), sds((rows, seq, hd), BF16), f((rows, seq, hd), BF16),
                       f((rows, seq, hd), BF16), accs, f((n, 8, LANES), F32)),
            in_specs=[SM, SM, VM, VM, VM, VM], out_specs=(HB, HB, VM, VM, VM, VM),
            scratch_shapes=[f(accs.shape, F32), DMA((2, rows // group))],
            input_output_aliases={4: 2, 5: 3},
            compiler_params=pltpu.CompilerParams(vmem_limit_bytes=16 * 2 ** 20),
            name='attn',
        )(write_pos, valid_len, q, kv, kb, vb)

        wide = width // n
        pair = (chunks, nx, hd // LANES, per * chunk, LANES)
        sums = (chunks, nx, chunk, wide)
        mls = (nx, 8, LANES)
        out = pl.pallas_call(
            functools.partial(out_kernel, n),
            out_shape=sds((rows, width), BF16),
            in_specs=[VM, VM, VM], out_specs=VM,
            scratch_shapes=[f(pair, F32), f(mls, F32), f((nx, LANES, 8), F32), f(pair, F32), f(mls, F32),
                            f(pair, F32), f(mls, F32), f((LANES, 8), F32),
                            f(sums, F32), f(sums, F32), f(sums, F32), f(sums, F32),
                            ] + [DMA((nx,))] * 4 + [DMA((chunks, nx))] * 12,
            compiler_params=pltpu.CompilerParams(collective_id=1, has_side_effects=True,
                                                 vmem_limit_bytes=20 * 2 ** 20),
            name='outp',
        )(acc, ml, w_out)
        return out, k_new.reshape(k_cache.shape), v_new.reshape(v_cache.shape)

    return jax.shard_map(local_step, mesh=mesh,
                         in_specs=(row_spec, P(), P(), P(), P('sp', None), cache_spec, cache_spec, len_spec, len_spec),
                         out_specs=(row_spec, cache_spec, cache_spec), check_vma=False)
```

time: 202 us -> 46.4 us (0.23)
  blocking collectives: 76.4 us -> 0 us
  waiting for transfers between devices: 60.4 us -> 0 us
  Pallas kernels: 0 us -> 44.8 us
  matrix products: 30.9 us -> 0 us
  between operations: 14.2 us -> 0.7 us
  other arithmetic: 11.2 us -> 0 us
  local copies, waits for them, and re-layouts: 7.97 us -> 0.81 us
    psum x1 -> x0, waiting for transfers between devices: 60.3 us -> none  [local_step(): packed = lax.psum(packed, 'sp')]
    psum x1 -> x0, blocking collectives: 52.3 us -> none  [local_step(): attn_out = lax.psum(partial_out, 'sp').astype(jnp.bfloat16)]
    pallas_call x0 -> x3, Pallas kernels: none -> 44.8 us  [the longest x1 26.9 us: local_step(): pl.pallas_call(functools.partial(out_kernel, n), out_shape=sds((rows, wid...]
    dot_general x6 -> x0, matrix products: 30.9 us -> none  [the longest x1 16.8 us: local_step(): jnp.dot(hidden, w_query, preferred_element_type=jnp.float32)]
    pmax x1 -> x0, blocking collectives: 24 us -> none  [local_step(): global_max = lax.pmax(local_max, 'sp')]
    select_n x1 -> x0, other arithmetic: 8.02 us -> none  [local_step(): jnp.where(at_pos, value_new.reshape(num_rows, 1, kv_heads, head_dim), v_c...]
    unnamed x18 -> x7, local copies, waits for them, and re-layouts: 5.22 us -> 0.81 us
  transfers between devices with their start and end apart: 1 -> 0, of which waited for: 1 -> 0; matrix products, arithmetic and copies ran while one was open for 0% -> 0% of each run, Pallas kernels for 0% -> 0%
where the time goes in v2:
time: 46.4 us; the launch traced here: 46.3 us
  Pallas kernels  44.8 us (97%)
  local copies, waits for them, and re-layouts  0.81 us (2%)
  between operations  0.7 us (2%)
    pallas_call x1, Pallas kernels, local_step(): pl.pallas_call(functools.partial(out_kernel, n), out_shape=sds((rows, wid...  26.9 us
    pallas_call x1, Pallas kernels, local_step(): pl.pallas_call(functools.partial(qkv_kernel, n), out_shape=(f((n, rows, c...  11.2 us
    pallas_call x1, Pallas kernels, local_step(): pl.pallas_call(functools.partial(attn_kernel, group, chunk, hd ** (-0.5))...  6.7 us

profile of v2, /device:TPU:97, one launch (start us, length us, event | category | flops | bytes accessed | tf_op | source)
XLA Modules:
  0.0 46.3 jit_solution(9685351900834994336)
XLA Ops:
  0.6 0.0 copy-start.1
  0.6 0.0 copy-start.2
  0.7 11.2 %qkv.1 = (bf16[8,64,512]{2,1,0:T(8,128)(2,1)S(1)}, f32[2,64,256]{2,1,0:T(8,128)S(1)}, bf16[64,256,256]{2,1,0:T(8,128)(2,1)S(1)}, bf16[64,256,256]{2,1,0:T(8,128)(2,1)S(1)}) custom-call(bf16[64,4096]{1,0:T(8,128)(2,1)} %hid_hbm.1, bf16[4096,4096]{1,0:T(8,128)(2,1)} %wq_hbm.1, bf16[4096,256]{1,0:T(8,128)(2,1)} %wk_hbm.1, bf16[4096,256]{1,0:T(8,128)(2,1)} %wv_hbm.1, ...), custom_call_target="tpu_custom_call" | custom-call | tf_op jit(solution)/shard_map/qkv/pallas_call | solution.py:334
  11.8 0.0 copy-done.1
  11.8 0.0 copy-done.2
  11.8 0.0 copy-start
  11.8 6.7 %attn.1 = (bf16[64,256,256]{2,1,0:T(8,128)(2,1)}, bf16[64,256,256]{2,1,0:T(8,128)(2,1)}, bf16[64,256,256]{2,1,0:T(8,128)(2,1)S(1)}, bf16[64,256,256]{2,1,0:T(8,1...) custom-call(s32[64]{0:T(128)S(1)} %copy-done.1, ...), custom_call_target="tpu_custom_call", output_to_operand_aliasing={{2}: (4, {}), {3}: (5, {})} | custom-call | tf_op jit(solution)/shard_map/attn/pallas_call | solution.py:347
  18.5 0.0 copy-done
  18.6 26.9 %outp.1 = bf16[64,4096]{1,0:T(8,128)(2,1)S(1)} custom-call(f32[2,1024,128]{2,1,0:T(8,128)S(1)} %get-tuple-element.15.acc_ref, f32[8,8,128]{2,1,0:T(8,128)S(1)} %get-tuple-element.16.ml_ref, bf16[512,4096]{1,0:T(8,128)(2,1)S(1)} %copy-done), custom_call_target="tpu_custom_call" | custom-call | tf_op jit(solution)/shard_map/outp/pallas_call | solution.py:362
  45.5 0.8 %copy.19 = bf16[64,4096]{1,0:T(8,128)(2,1)} copy(bf16[64,4096]{1,0:T(8,128)(2,1)S(1)} %outp.1) | data formatting | bytes 1048576
Async XLA Ops:
  0.6 11.2 %copy-start.1 = (s32[64]{0:T(128)S(1)}, s32[64]{0:T(128)}, u32[]{:S(2)}) copy-start(s32[64]{0:T(128)} %wp.1) | copy-start | bytes 772
  0.6 11.2 %copy-start.2 = (s32[64]{0:T(128)S(1)}, s32[64]{0:T(128)}, u32[]{:S(2)}) copy-start(s32[64]{0:T(128)} %vl.1) | copy-start | bytes 772
  11.8 6.7 %copy-start = (bf16[512,4096]{1,0:T(8,128)(2,1)S(1)}, bf16[512,4096]{1,0:T(8,128)(2,1)}, u32[]{:S(2)}) copy-start(bf16[512,4096]{1,0:T(8,128)(2,1)} %w_ref.1) | copy-start | bytes 12582916

commit v3 on v2

--- a/solution.py
+++ b/solution.py
@@ -93,12 +93,61 @@
         cp.wait()
 
 
-def attn_kernel(group, chunk, scale, wp, vl, q_ref, kv_ref, k_in, v_in, ko_hbm, vo_hbm, kb, vb, acc_ref, ml_ref,
-                qs, osem):
+def stage_q(qs, q_ref, first, last, chunk, hd):
+    per = q_ref.shape[2] // hd
+    heads = q_ref.shape[0] * per
+    for t in range(first, last):
+        for h in range(heads):
+            to = ((t - first) * heads + h) * chunk
+            for z in range(hd // LANES):
+                lo = (h % per) * hd + z * LANES
+                qs[z, to:to + chunk, :] = q_ref[h // per, t * chunk:(t + 1) * chunk, lo:lo + LANES].astype(F32)
+
+
+def attend(qs, kb, vb, vl, acc, b0, at0, group, chunk, heads, base, scale, m_all, l_all):
+    seq, hd = kb.shape[1:]
+    halves = hd // LANES
+    pos_iota = lax.broadcasted_iota(jnp.int32, (heads, seq), 1)
+    lane_iota = lax.broadcasted_iota(jnp.int32, (heads, LANES), 1)
+    scores = []
+    for r in range(group):
+        qb = jnp.concatenate([qs[z, pl.ds(at0 + r, heads, stride=chunk), :] for z in range(halves)], axis=1)
+        scores.append(lax.dot_general(qb.astype(BF16), kb[b0 + r], (((1,), (1,)), ((), ())),
+                                      preferred_element_type=F32))
+    probs = []
+    for r in range(group):
+        valid = pos_iota < vl[b0 + r] - base
+        s = jnp.where(valid, scores[r] * scale, NEG)
+        m = jnp.max(s, axis=1, keepdims=True)
+        p = jnp.where(valid, jnp.exp(s - m), 0.0)
+        l = jnp.sum(p, axis=1, keepdims=True)
+        here = lane_iota == b0 + r
+        m_all = jnp.where(here, m, m_all)
+        l_all = jnp.where(here, l, l_all)
+        probs.append(p.astype(BF16))
+    for r in range(group):
+        o = jnp.dot(probs[r], vb[b0 + r], preferred_element_type=F32)
+        for z in range(halves):
+            acc[z, pl.ds(at0 + r, heads, stride=chunk), :] = o[:, z * LANES:(z + 1) * LANES]
+    return m_all, l_all
+
+
+def attend_rows(qs, kb, vb, vl, acc, first, last, group, chunk, heads, base, scale):
+    def step(g, carry):
+        i0 = g * group
+        at0 = (i0 // chunk) * (heads * chunk) + lax.rem(i0, chunk)
+        return attend(qs, kb, vb, vl, acc, first * chunk + i0, at0, group, chunk, heads, base, scale, *carry)
+
+    init = (jnp.full((heads, LANES), NEG, F32), jnp.zeros((heads, LANES), F32))
+    return lax.fori_loop(0, (last - first) * chunk // group, step, init)
+
+
+def attn_kernel(group, chunk, early, scale, wp, vl, q_ref, kv_ref, k_in, v_in, ko_hbm, vo_hbm, kb, vb, acc_ref,
+                ml_ref, qs, osem):
     del k_in, v_in
     rows, seq, hd = kb.shape
-    heads = acc_ref.shape[1] // rows
-    halves = hd // LANES
+    heads = q_ref.shape[0] * (q_ref.shape[2] // hd)
+    per = heads // ml_ref.shape[0]
     steps = rows // group
     base = lax.axis_index('sp') * seq
 
@@ -107,62 +156,27 @@
         return (pltpu.make_async_copy(kb.at[s], ko_hbm.at[s], osem.at[0, g]),
                 pltpu.make_async_copy(vb.at[s], vo_hbm.at[s], osem.at[1, g]))
 
-    per = q_ref.shape[2] // hd
     row_iota = lax.broadcasted_iota(jnp.int32, (16, hd), 0)
 
-    def put(buf, i, b, pos):
-        start = pl.multiple_of((jnp.clip(pos, 0, seq - 1) // 16) * 16, 16)
-        slab = buf[b, pl.ds(start, 16), :].astype(F32)
-        row = jnp.broadcast_to(kv_ref[i, pl.ds(b, 1), :], slab.shape)
-        buf[b, pl.ds(start, 16), :] = jnp.where(row_iota == pos - start, row, slab).astype(BF16)
-
     def update(g, carry):
+        slabs = []
         for r in range(group):
-            pos = wp[g * group + r] - base
-            put(kb, 0, g * group + r, pos)
-            put(vb, 1, g * group + r, pos)
+            b = g * group + r
+            pos = wp[b] - base
+            start = pl.multiple_of((jnp.clip(pos, 0, seq - 1) // 16) * 16, 16)
+            for i, buf in enumerate((kb, vb)):
+                row = jnp.broadcast_to(kv_ref[i, pl.ds(b, 1), :], (16, hd))
+                slab = buf[b, pl.ds(start, 16), :].astype(F32)
+                slabs.append((buf, b, start, jnp.where(row_iota == pos - start, row, slab).astype(BF16)))
+        for buf, b, start, slab in slabs:
+            buf[b, pl.ds(start, 16), :] = slab
         for cp in store(g):
             cp.start()
         return carry
 
     lax.fori_loop(0, steps, update, 0)
-    for h in range(heads):
-        for z in range(halves):
-            lo = (h % per) * hd + z * LANES
-            for t in range(rows // chunk):
-                to = (t * heads + h) * chunk
-                qs[z, to:to + chunk, :] = q_ref[h // per, t * chunk:(t + 1) * chunk, lo:lo + LANES].astype(F32)
-
-    pos_iota = lax.broadcasted_iota(jnp.int32, (heads, seq), 1)
-    lane_iota = lax.broadcasted_iota(jnp.int32, (heads, LANES), 1)
-
-    def step(g, carry):
-        m_all, l_all = carry
-        b0 = g * group
-        at0 = (b0 // chunk) * (heads * chunk) + lax.rem(b0, chunk)
-        scores = []
-        for r in range(group):
-            qb = jnp.concatenate([qs[z, pl.ds(at0 + r, heads, stride=chunk), :] for z in range(halves)], axis=1)
-            scores.append(lax.dot_general(qb.astype(BF16), kb[b0 + r], (((1,), (1,)), ((), ())),
-                                          preferred_element_type=F32))
-        probs = []
-        for r in range(group):
-            valid = pos_iota < vl[b0 + r] - base
-            s = jnp.where(valid, scores[r] * scale, NEG)
-            m = jnp.max(s, axis=1, keepdims=True)
-            p = jnp.where(valid, jnp.exp(s - m), 0.0)
-            l = jnp.sum(p, axis=1, keepdims=True)
-            here = lane_iota == b0 + r
-            m_all = jnp.where(here, m, m_all)
-            l_all = jnp.where(here, l, l_all)
-            probs.append(p.astype(BF16))
-        for r in range(group):
-            o = jnp.dot(probs[r], vb[b0 + r], preferred_element_type=F32)
-            for z in range(halves):
-                acc_ref[z, pl.ds(at0 + r, heads, stride=chunk), :] = o[:, z * LANES:(z + 1) * LANES]
-        return m_all, l_all
-
-    m_all, l_all = lax.fori_loop(0, steps, step, (jnp.full((heads, LANES), NEG, F32), jnp.zeros((heads, LANES), F32)))
+    stage_q(qs, q_ref, 0, early, chunk, hd)
+    m_all, l_all = attend_rows(qs, kb, vb, vl, acc_ref, 0, early, group, chunk, heads, base, scale)
     for i in range(ml_ref.shape[0]):
         ml_ref[i, 0:per, :] = m_all[i * per:(i + 1) * per]
         ml_ref[i, per:2 * per, :] = l_all[i * per:(i + 1) * per]
@@ -171,8 +185,9 @@
             cp.wait()
 
 
-def out_kernel(n, acc_ref, ml_ref, w_ref, out_ref, ra, rml, ca, sb, sml, rb, rbml, cb, sd, rd, se, re,
-               amsend, amrecv, bmsend, bmrecv, asend, arecv, bsend, brecv, dsend, drecv, esend, erecv,
+def out_kernel(n, group, scale, vl, q_ref, kb, vb, acc_ref, ml_in, w_hbm, out_ref, qs, acc_own, ml_ref, wv,
+               ra, rml, ca, sb, sml, rb, rbml, cb, sd, rd, se, re,
+               wsem, amsend, amrecv, bmsend, bmrecv, asend, arecv, bsend, brecv, dsend, drecv, esend, erecv,
                fsend, frecv, gsend, grecv):
     nx = n // 2
     me = lax.axis_index('sp')
@@ -183,6 +198,8 @@
     chunks, blk = ra.shape[0], ra.shape[3]
     chunk = out_ref.shape[0] // chunks
     per = blk // chunk
+    heads = per * n
+    early = acc_ref.shape[1] // (heads * chunk)
     far = [2, 1, 3] if nx == 4 else list(range(1, nx))
     near = [1, 3, 2] if nx == 4 else list(range(1, nx))
     order = far + [0]
@@ -194,10 +211,24 @@
     peers = [2 * chip(d) + c for d in range(1, nx)] + [partner]
     for peer in peers:
         pl.semaphore_signal(bar, inc=1, device_id=sp_dev(peer), device_id_type=MESH)
+    wloads = []
+    for j in range(n):
+        cp = pltpu.make_async_copy(w_hbm.at[:, j * wide:(j + 1) * wide], wv.at[j], wsem.at[j])
+        cp.start()
+        wloads.append(cp)
+    stage_q(qs, q_ref, early, chunks, chunk, kb.shape[2])
+    m_all, l_all = attend_rows(qs, kb, vb, vl, acc_own, early, chunks, group, chunk, heads, me * kb.shape[1], scale)
+    late = lax.broadcasted_iota(jnp.int32, (per, LANES), 1) >= early * chunk
+    for i in range(n):
+        for k, u in enumerate((m_all, l_all)):
+            r = slice(k * per, (k + 1) * per)
+            ml_ref[i, r, :] = jnp.where(late, u[i * per:(i + 1) * per], ml_in[i, r, :])
     pl.semaphore_wait(bar, len(peers))
 
     def acc_at(t, j):
-        return pl.ds(pl.multiple_of((t * n + j) * blk, blk), blk)
+        if t < early:
+            return acc_ref, pl.multiple_of((t * n + j) * blk, blk)
+        return acc_own, pl.multiple_of(((t - early) * n + j) * blk, blk)
 
     pending = []
 
@@ -213,31 +244,37 @@
         go(ml_ref.at[2 * chip(d) + 1 - c], rml.at[d], amsend.at[d], amrecv.at[d], partner)
     for t in range(chunks):
         for d in order:
-            go(acc_ref.at[:, acc_at(t, 2 * chip(d) + 1 - c)], ra.at[t, d], asend.at[t, d], arecv.at[t, d], partner)
+            src, at = acc_at(t, 2 * chip(d) + 1 - c)
+            go(src.at[:, pl.ds(at, blk)], ra.at[t, d], asend.at[t, d], arecv.at[t, d], partner)
     for d in order:
-        j = 2 * chip(d) + c
-        landed(ml_ref.at[j], rml.at[d], amsend.at[d], amrecv.at[d])
-        mine, theirs = ml_ref[j], rml[d]
+        landed(ml_ref.at[0], rml.at[d], amsend.at[d], amrecv.at[d])
+    for d in order:
+        mine, theirs = ml_ref[2 * chip(d) + c], rml[d]
         m = jnp.maximum(mine[0:per], theirs[0:per])
         fa, fb = jnp.exp(mine[0:per] - m), jnp.exp(theirs[0:per] - m)
         l = fa * mine[per:2 * per] + fb * theirs[per:2 * per]
         ca[d] = jnp.transpose(jnp.concatenate([fa, fb, m, l], axis=0))
         sml[d, 0:per, :] = m
         sml[d, per:2 * per, :] = l
-        if d:
-            go(sml.at[d], rbml.at[d], bmsend.at[d], bmrecv.at[d], j)
-    for t in range(chunks):
-        for d in order:
-            j = 2 * chip(d) + c
+    for d in far:
+        go(sml.at[d], rbml.at[d], bmsend.at[d], bmrecv.at[d], 2 * chip(d) + c)
+
+    def pair(t):
+        for d in order:
             landed(ra.at[t, d], ra.at[t, d], asend.at[t, d], arecv.at[t, d])
+        for d in order:
+            src, at = acc_at(t, 2 * chip(d) + c)
+            f = ca[d, t * chunk:(t + 1) * chunk, :]
             for h in range(per):
                 r = slice(h * chunk, (h + 1) * chunk)
-                f = ca[d, t * chunk:(t + 1) * chunk, :]
                 for z in range(halves):
-                    own = acc_ref[z, pl.ds(pl.multiple_of((t * n + j) * blk + h * chunk, chunk), chunk), :]
+                    own = src[z, pl.ds(at + h * chunk, chunk), :]
                     sb[t, d, z, r, :] = own * f[:, h:h + 1] + ra[t, d, z, r, :] * f[:, per + h:per + h + 1]
-            if d:
-                go(sb.at[t, d], rb.at[t, d], bsend.at[t, d], brecv.at[t, d], j)
+        for d in far:
+            go(sb.at[t, d], rb.at[t, d], bsend.at[t, d], brecv.at[t, d], 2 * chip(d) + c)
+
+    for t in range(chunks):
+        pair(t)
     for d in range(1, nx):
         landed(sml.at[d], rbml.at[d], bmsend.at[d], bmrecv.at[d])
     mls = [sml[0]] + [rbml[d] for d in range(1, nx)]
@@ -245,9 +282,8 @@
     fs = [jnp.exp(u[0:per] - m) for u in mls]
     l = sum(f * u[per:2 * per] for f, u in zip(fs, mls))
     cb[...] = jnp.transpose(jnp.concatenate([f / l for f in fs], axis=0))
-
-    def w_at(j):
-        return w_ref[:, pl.ds(pl.multiple_of(j * wide, wide), wide)]
+    for cp in wloads:
+        cp.wait()
 
     def out_at(t, j):
         return out_ref.at[pl.ds(t * chunk, chunk), pl.ds(pl.multiple_of(j * wide, wide), wide)]
@@ -256,23 +292,27 @@
         for d in range(1, nx):
             landed(sb.at[t, d], rb.at[t, d], bsend.at[t, d], brecv.at[t, d])
         f = cb[t * chunk:(t + 1) * chunk, :]
-        heads = []
+        parts = []
         for h in range(per):
             r = slice(h * chunk, (h + 1) * chunk)
             for z in range(halves):
                 terms = [sb[t, 0, z, r, :]] + [rb[t, d, z, r, :] for d in range(1, nx)]
-                heads.append(sum(u * f[:, d * per + h:d * per + h + 1] for d, u in enumerate(terms)))
-        attn = jnp.concatenate(heads, axis=1).astype(BF16)
-        for d in order:
-            sd[t, d] = jnp.dot(attn, w_at(2 * chip(d) + 1 - c), preferred_element_type=F32)
+                parts.append(sum(u * f[:, d * per + h:d * per + h + 1] for d, u in enumerate(terms)))
+        attn = jnp.concatenate(parts, axis=1).astype(BF16)
+        for d in order:
+            sd[t, d] = jnp.dot(attn, wv[2 * chip(d) + 1 - c], preferred_element_type=F32)
+        for d in order:
             go(sd.at[t, d], rd.at[t, d], dsend.at[t, d], drecv.at[t, d], partner)
         for d in order:
-            se[t, d] = jnp.dot(attn, w_at(2 * chip(d) + c), preferred_element_type=F32)
+            se[t, d] = jnp.dot(attn, wv[2 * chip(d) + c], preferred_element_type=F32)
+
+    def reduce(t):
         for d in order:
             landed(sd.at[t, d], rd.at[t, d], dsend.at[t, d], drecv.at[t, d])
+        for d in order:
             se[t, d] = se[t, d] + rd[t, d]
-            if d:
-                go(se.at[t, d], re.at[t, d], esend.at[t, d], erecv.at[t, d], 2 * chip(d) + c)
+        for d in far:
+            go(se.at[t, d], re.at[t, d], esend.at[t, d], erecv.at[t, d], 2 * chip(d) + c)
 
     def finish(t):
         for d in range(1, nx):
@@ -289,16 +329,17 @@
             landed(out_at(t, me), out_at(t, src), fsend.at[t, d], frecv.at[t, d])
             go(out_at(t, src), out_at(t, src), gsend.at[t, d], grecv.at[t, d], partner)
 
-    for t in range(chunks):
+    project(0)
+    for t in range(1, chunks):
         project(t)
-        if t >= 2:
-            finish(t - 2)
-    finish(chunks - 2)
-    for t in range(chunks - 2):
+        reduce(t - 1)
+    reduce(chunks - 1)
+    for t in range(chunks - 1):
+        finish(t)
+    forward(0)
+    finish(chunks - 1)
+    for t in range(1, chunks):
         forward(t)
-    finish(chunks - 1)
-    forward(chunks - 2)
-    forward(chunks - 1)
     for t in range(chunks):
         for d in [0] + near:
             src = 2 * chip(nx - d if d else 0) + 1 - c
@@ -343,34 +384,38 @@
             name='qkv',
         )(hidden, w_query, w_key, w_value, k3, v3)
 
-        accs = f((hd // LANES, heads * rows, LANES), F32)
-        k_new, v_new, _, _, acc, ml = pl.pallas_call(
-            functools.partial(attn_kernel, group, chunk, hd ** -0.5),
+        early = chunks - 1
+        halves = hd // LANES
+        k_new, v_new, kb, vb, acc, ml = pl.pallas_call(
+            functools.partial(attn_kernel, group, chunk, early, hd ** -0.5),
             out_shape=(sds((rows, seq, hd), BF16), sds((rows, seq, hd), BF16), f((rows, seq, hd), BF16),
-                       f((rows, seq, hd), BF16), accs, f((n, 8, LANES), F32)),
+                       f((rows, seq, hd), BF16), f((halves, early * heads * chunk, LANES), F32),
+                       f((n, 8, LANES), F32)),
             in_specs=[SM, SM, VM, VM, VM, VM], out_specs=(HB, HB, VM, VM, VM, VM),
-            scratch_shapes=[f(accs.shape, F32), DMA((2, rows // group))],
+            scratch_shapes=[f((halves, early * heads * chunk, LANES), F32), DMA((2, rows // group))],
             input_output_aliases={4: 2, 5: 3},
             compiler_params=pltpu.CompilerParams(vmem_limit_bytes=16 * 2 ** 20),
             name='attn',
         )(write_pos, valid_len, q, kv, kb, vb)
 
         wide = width // n
-        pair = (chunks, nx, hd // LANES, per * chunk, LANES)
+        pair = (chunks, nx, halves, per * chunk, LANES)
         sums = (chunks, nx, chunk, wide)
         mls = (nx, 8, LANES)
+        own = (halves, (chunks - early) * heads * chunk, LANES)
         out = pl.pallas_call(
-            functools.partial(out_kernel, n),
+            functools.partial(out_kernel, n, group, hd ** -0.5),
             out_shape=sds((rows, width), BF16),
-            in_specs=[VM, VM, VM], out_specs=VM,
-            scratch_shapes=[f(pair, F32), f(mls, F32), f((nx, LANES, 8), F32), f(pair, F32), f(mls, F32),
+            in_specs=[SM, VM, VM, VM, VM, VM, HB], out_specs=VM,
+            scratch_shapes=[f(own, F32), f(own, F32), f((n, 8, LANES), F32), f((n, w_out.shape[0], wide), BF16),
+                            f(pair, F32), f(mls, F32), f((nx, LANES, 8), F32), f(pair, F32), f(mls, F32),
                             f(pair, F32), f(mls, F32), f((LANES, 8), F32),
                             f(sums, F32), f(sums, F32), f(sums, F32), f(sums, F32),
-                            ] + [DMA((nx,))] * 4 + [DMA((chunks, nx))] * 12,
+                            DMA((n,))] + [DMA((nx,))] * 4 + [DMA((chunks, nx))] * 12,
             compiler_params=pltpu.CompilerParams(collective_id=1, has_side_effects=True,
                                                  vmem_limit_bytes=20 * 2 ** 20),
             name='outp',
-        )(acc, ml, w_out)
+        )(valid_len, q, kb, vb, acc, ml, pltpu.with_memory_space_constraint(w_out, pltpu.HBM))
         return out, k_new.reshape(k_cache.shape), v_new.reshape(v_cache.shape)
 
     return jax.shard_map(local_step, mesh=mesh,

time: 46.4 us -> 45.9 us (0.989)
  Pallas kernels: 44.8 us -> 44.3 us
    pallas_call x2, Pallas kernels: 33.6 us -> 33.1 us  [the longest x1 26.5 us: local_step(): pl.pallas_call(functools.partial(out_kernel, n, group, hd ** (-0.5)), out...]
where the time goes in v3:
time: 45.9 us; the launch traced here: 45.8 us
  Pallas kernels  44.3 us (97%)
  local copies, waits for them, and re-layouts  0.8 us (2%)
  between operations  0.69 us (2%)
    pallas_call x1, Pallas kernels, local_step(): pl.pallas_call(functools.partial(out_kernel, n, group, hd ** (-0.5)), out...  26.5 us
    pallas_call x1, Pallas kernels, local_step(): pl.pallas_call(functools.partial(qkv_kernel, n), out_shape=(f((n, rows, c...  11.2 us
    pallas_call x1, Pallas kernels, local_step(): pl.pallas_call(functools.partial(attn_kernel, group, chunk, early, hd **...  6.6 us

profile of v3, /device:TPU:97, one launch (start us, length us, event | category | flops | bytes accessed | tf_op | source)
XLA Modules:
  0.0 45.8 jit_solution(17343019041453853746)
XLA Ops:
  0.6 0.0 copy-start
  0.6 0.0 copy-start.1
  0.7 11.2 %qkv.1 = (bf16[8,64,512]{2,1,0:T(8,128)(2,1)S(1)}, f32[2,64,256]{2,1,0:T(8,128)S(1)}, bf16[64,256,256]{2,1,0:T(8,128)(2,1)S(1)}, bf16[64,256,256]{2,1,0:T(8,128)(2,1)S(1)}) custom-call(bf16[64,4096]{1,0:T(8,128)(2,1)} %hid_hbm.1, bf16[4096,4096]{1,0:T(8,128)(2,1)} %wq_hbm.1, bf16[4096,256]{1,0:T(8,128)(2,1)} %wk_hbm.1, bf16[4096,256]{1,0:T(8,128)(2,1)} %wv_hbm.1, ...), custom_call_target="tpu_custom_call" | custom-call | tf_op jit(solution)/shard_map/qkv/pallas_call | solution.py:375
  11.8 0.0 copy-done
  11.8 0.0 copy-done.1
  11.8 6.6 %attn.1 = (bf16[64,256,256]{2,1,0:T(8,128)(2,1)}, bf16[64,256,256]{2,1,0:T(8,128)(2,1)}, bf16[64,256,256]{2,1,0:T(8,128)(2,1)S(1)}, bf16[64,256,256]{2,1,0:T(8,1...) custom-call(s32[64]{0:T(128)S(1)} %copy-done.1, ...), custom_call_target="tpu_custom_call", output_to_operand_aliasing={{2}: (4, {}), {3}: (5, {})} | custom-call | tf_op jit(solution)/shard_map/attn/pallas_call | solution.py:389
  18.4 26.5 %outp.1 = bf16[64,4096]{1,0:T(8,128)(2,1)S(1)} custom-call(s32[64]{0:T(128)S(1)} %copy-done, bf16[8,64,512]{2,1,0:T(8,128)(2,1)S(1)} %get-tuple-element.13.q_ref, bf16[64,256,256]{2,1,0:T(8,128)(2,1)S(1)} %get-tuple-element.17.kb, bf16[64,256,256]{2,1,0:T(8,128)(2,1)S(1)} %get-tuple-element.18.vb, f32[2,768,128]{2,1,0:T(8,128)S(1)} %get-tuple-element.19.acc_ref, ...), custom_call_target="tpu_custom_call" | custom-call | tf_op jit(solution)/shard_map/outp/pallas_call | solution.py:406
  45.0 0.8 %copy.19 = bf16[64,4096]{1,0:T(8,128)(2,1)} copy(bf16[64,4096]{1,0:T(8,128)(2,1)S(1)} %outp.1) | data formatting | bytes 1048576
Async XLA Ops:
  0.6 11.2 %copy-start = (s32[64]{0:T(128)S(1)}, s32[64]{0:T(128)}, u32[]{:S(2)}) copy-start(s32[64]{0:T(128)} %vl.3) | copy-start | bytes 772
  0.6 11.2 %copy-start.1 = (s32[64]{0:T(128)S(1)}, s32[64]{0:T(128)}, u32[]{:S(2)}) copy-start(s32[64]{0:T(128)} %wp.1) | copy-start | bytes 772

commit v4 on v3

v4 whole, which is shorter than its diff:
```python
import functools

import jax
import jax.numpy as jnp
from jax import lax
from jax.experimental import pallas as pl
from jax.experimental.pallas import tpu as pltpu
from jax.sharding import PartitionSpec as P

MESH = pl.DeviceIdType.MESH
NEG = -3.4e38
LANES = 128
F32 = jnp.float32
BF16 = jnp.bfloat16


def sp_dev(i):
    return {'sp': i}


def rcopy(src, dst, ss, rs, dev):
    return pltpu.make_async_remote_copy(src_ref=src, dst_ref=dst, send_sem=ss, recv_sem=rs,
                                        device_id=sp_dev(dev), device_id_type=MESH)


def qkv_kernel(n, hid_hbm, wq_hbm, wk_hbm, wv_hbm, k_hbm, v_hbm, q_ref, kv_ref, kb, vb,
               hid, wq, wkv, hsem, wsem, csem, ssem, rsem, psend, precv):
    nx = n // 2
    me = lax.axis_index('sp')
    x, c = me // 2, lax.rem(me, 2)
    cols = wq.shape[2]
    own = me
    opp = 2 * lax.rem(x + nx // 2, nx) + c
    partner = 2 * x + 1 - c
    ch = pltpu.make_async_copy(hid_hbm, hid, hsem)
    ch.start()
    loads = []
    for i, blk in enumerate((own, opp)):
        cp = pltpu.make_async_copy(wq_hbm.at[:, pl.ds(pl.multiple_of(blk * cols, cols), cols)], wq.at[i], wsem.at[i])
        cp.start()
        loads.append(cp)
    near = [lax.rem(x + d, nx) for d in (1, nx - 1)]
    bar = pltpu.get_barrier_semaphore()
    peers = [2 * t + u for t in near for u in range(2)] + [partner]
    for peer in peers:
        pl.semaphore_signal(bar, inc=1, device_id=sp_dev(peer), device_id_type=MESH)
    pick = [pltpu.make_async_copy(w, wkv, wsem.at[2]) for w in (wk_hbm, wv_hbm)]
    for i in range(2):
        @pl.when(c == i)
        def _():
            pick[i].start()
    ch.wait()
    loads[0].wait()
    parts = csem.shape[1]
    step = kb.shape[0] // parts
    caches = []
    for g in range(parts):
        for i, (src, dst) in enumerate(((k_hbm, kb), (v_hbm, vb))):
            cp = pltpu.make_async_copy(src.at[pl.ds(g * step, step)], dst.at[pl.ds(g * step, step)], csem.at[i, g])
            cp.start()
            caches.append(cp)

    def project(w):
        return jnp.dot(hid[...], w, preferred_element_type=F32).astype(BF16)

    q_ref[own] = project(wq[0])
    pl.semaphore_wait(bar, len(peers))
    sends = []
    for d in range(2):
        for t in range(2):
            sends.append(rcopy(q_ref.at[own], q_ref.at[own], ssem.at[d, t], rsem.at[d, c], 2 * near[d] + t))
    sends.append(rcopy(q_ref.at[own], q_ref.at[own], psend.at[0], precv.at[0], partner))
    for s in sends:
        s.start()
    loads[1].wait()
    q_ref[opp] = project(wq[1])
    sends.append(rcopy(q_ref.at[opp], q_ref.at[opp], psend.at[1], precv.at[1], partner))
    sends[-1].start()
    pick[0].wait()
    kv_ref[c] = project(wkv[...])
    sends.append(rcopy(kv_ref.at[c], kv_ref.at[c], psend.at[2], precv.at[2], partner))
    sends[-1].start()
    for s in sends:
        s.wait_send()
    popp = 2 * lax.rem(x + nx // 2, nx) + 1 - c
    rcopy(q_ref.at[own], q_ref.at[partner], psend.at[0], precv.at[0], partner).wait_recv()
    rcopy(q_ref.at[own], q_ref.at[popp], psend.at[1], precv.at[1], partner).wait_recv()
    rcopy(kv_ref.at[c], kv_ref.at[1 - c], psend.at[2], precv.at[2], partner).wait_recv()
    for d in range(2):
        for t in range(2):
            rcopy(q_ref.at[own], q_ref.at[2 * near[1 - d] + t], ssem.at[d, t], rsem.at[d, t], partner).wait_recv()
    for cp in caches:
        cp.wait()


def stage_q(qs, q_ref, t, chunk, hd):
    per = q_ref.shape[2] // hd
    for h in range(q_ref.shape[0] * per):
        for z in range(hd // LANES):
            lo = (h % per) * hd + z * LANES
            qs[z, h * chunk:(h + 1) * chunk, :] = q_ref[h // per, t * chunk:(t + 1) * chunk, lo:lo + LANES].astype(F32)


def attend(qs, kb, vb, vl, acc, b0, at0, group, chunk, heads, base, scale, m_all, l_all):
    seq, hd = kb.shape[1:]
    halves = hd // LANES
    pos_iota = lax.broadcasted_iota(jnp.int32, (heads, seq), 1)
    lane_iota = lax.broadcasted_iota(jnp.int32, (heads, LANES), 1)
    scores = []
    for r in range(group):
        qb = jnp.concatenate([qs[z, pl.ds(at0 + r, heads, stride=chunk), :] for z in range(halves)], axis=1)
        scores.append(lax.dot_general(qb.astype(BF16), kb[b0 + at0 + r], (((1,), (1,)), ((), ())),
                                      preferred_element_type=F32))
    probs = []
    for r in range(group):
        valid = pos_iota < vl[b0 + at0 + r] - base
        s = jnp.where(valid, scores[r] * scale, NEG)
        m = jnp.max(s, axis=1, keepdims=True)
        p = jnp.where(valid, jnp.exp(s - m), 0.0)
        l = jnp.sum(p, axis=1, keepdims=True)
        here = lane_iota == at0 + r
        m_all = jnp.where(here, m, m_all)
        l_all = jnp.where(here, l, l_all)
        probs.append(p.astype(BF16))
    for r in range(group):
        o = jnp.dot(probs[r], vb[b0 + at0 + r], preferred_element_type=F32)
        for z in range(halves):
            acc[z, pl.ds(at0 + r, heads, stride=chunk), :] = o[:, z * LANES:(z + 1) * LANES]
    return m_all, l_all


def attn_out_kernel(n, group, scale, vl, q_ref, kb, vb, w_hbm, out_ref, qs, acc, ml, wv,
                    ra, rml, sb, sml, rb, rbml, sd, rd, se, re,
                    wsem, amsend, amrecv, bmsend, bmrecv, asend, arecv, bsend, brecv, dsend, drecv, esend, erecv,
                    fsend, frecv, gsend, grecv):
    nx = n // 2
    me = lax.axis_index('sp')
    x, c = me // 2, lax.rem(me, 2)
    partner = 2 * x + 1 - c
    wide = out_ref.shape[1] // n
    chunks, halves = acc.shape[:2]
    blk = acc.shape[2] // n
    chunk = out_ref.shape[0] // chunks
    per = blk // chunk
    heads = per * n
    hd = kb.shape[2]
    far = [2, 1, 3] if nx == 4 else list(range(1, nx))
    near = [1, 3, 2] if nx == 4 else list(range(1, nx))
    order = far + [0]

    def chip(d):
        return lax.rem(x + d, nx)

    bar = pltpu.get_barrier_semaphore()
    peers = [2 * chip(d) + c for d in range(1, nx)] + [partner]
    for peer in peers:
        pl.semaphore_signal(bar, inc=1, device_id=sp_dev(peer), device_id_type=MESH)
    wloads = []
    for j in range(n):
        cp = pltpu.make_async_copy(w_hbm.at[:, j * wide:(j + 1) * wide], wv.at[j], wsem.at[j])
        cp.start()
        wloads.append(cp)

    pending = []

    def go(*args):
        cp = rcopy(*args)
        cp.start()
        pending.append(cp)

    def landed(*args):
        rcopy(*args, partner).wait_recv()

    def acc_at(j):
        return pl.multiple_of(j * blk, blk)

    def local(t):
        stage_q(qs.at[t], q_ref, t, chunk, hd)

        def step(g, carry):
            return attend(qs.at[t], kb, vb, vl, acc.at[t], t * chunk, g * group, group, chunk, heads,
                          me * kb.shape[1], scale, *carry)

        init = (jnp.full((heads, LANES), NEG, F32), jnp.zeros((heads, LANES), F32))
        m_all, l_all = lax.fori_loop(0, chunk // group, step, init)
        for i in range(n):
            ml[t, i, 0:per, :] = m_all[i * per:(i + 1) * per]
            ml[t, i, per:2 * per, :] = l_all[i * per:(i + 1) * per]

    def share(t):
        for d in order:
            j = 2 * chip(d) + 1 - c
            go(ml.at[t, j], rml.at[t, d], amsend.at[t, d], amrecv.at[t, d], partner)
            go(acc.at[t, :, pl.ds(acc_at(j), blk)], ra.at[t, d], asend.at[t, d], arecv.at[t, d], partner)

    def pair(t):
        for d in order:
            landed(ml.at[t, 0], rml.at[t, d], amsend.at[t, d], amrecv.at[t, d])
            landed(ra.at[t, d], ra.at[t, d], asend.at[t, d], arecv.at[t, d])
        for d in order:
            j = 2 * chip(d) + c
            mine, theirs = ml[t, j], rml[t, d]
            m = jnp.maximum(mine[0:per], theirs[0:per])
            fa, fb = jnp.exp(mine[0:per] - m), jnp.exp(theirs[0:per] - m)
            l = fa * mine[per:2 * per] + fb * theirs[per:2 * per]
            f = jnp.transpose(jnp.concatenate([fa, fb, m, l], axis=0))[0:chunk]
            sml[t, d, 0:per, :] = m
            sml[t, d, per:2 * per, :] = l
            for h in range(per):
                r = slice(h * chunk, (h + 1) * chunk)
                for z in range(halves):
                    own = acc[t, z, pl.ds(acc_at(j) + h * chunk, chunk), :]
                    sb[t, d, z, r, :] = own * f[:, h:h + 1] + ra[t, d, z, r, :] * f[:, per + h:per + h + 1]
        for d in far:
            j = 2 * chip(d) + c
            go(sml.at[t, d], rbml.at[t, d], bmsend.at[t, d], bmrecv.at[t, d], j)
            go(sb.at[t, d], rb.at[t, d], bsend.at[t, d], brecv.at[t, d], j)

    def out_at(t, j):
        return out_ref.at[pl.ds(t * chunk, chunk), pl.ds(pl.multiple_of(j * wide, wide), wide)]

    def project(t):
        for d in range(1, nx):
            landed(sml.at[t, d], rbml.at[t, d], bmsend.at[t, d], bmrecv.at[t, d])
            landed(sb.at[t, d], rb.at[t, d], bsend.at[t, d], brecv.at[t, d])
        mls = [sml[t, 0]] + [rbml[t, d] for d in range(1, nx)]
        m = functools.reduce(jnp.maximum, [u[0:per] for u in mls])
        fs = [jnp.exp(u[0:per] - m) for u in mls]
        l = sum(f * u[per:2 * per] for f, u in zip(fs, mls))
        f = jnp.transpose(jnp.concatenate([f / l for f in fs], axis=0))[0:chunk]
        parts = []
        for h in range(per):
            r = slice(h * chunk, (h + 1) * chunk)
            for z in range(halves):
                terms = [sb[t, 0, z, r, :]] + [rb[t, d, z, r, :] for d in range(1, nx)]
                parts.append(sum(u * f[:, d * per + h:d * per + h + 1] for d, u in enumerate(terms)))
        attn = jnp.concatenate(parts, axis=1).astype(BF16)
        for d in order:
            sd[t, d] = jnp.dot(attn, wv[2 * chip(d) + 1 - c], preferred_element_type=F32)
        for d in order:
            go(sd.at[t, d], rd.at[t, d], dsend.at[t, d], drecv.at[t, d], partner)
        for d in order:
            se[t, d] = jnp.dot(attn, wv[2 * chip(d) + c], preferred_element_type=F32)

    def reduce(t):
        for d in order:
            landed(sd.at[t, d], rd.at[t, d], dsend.at[t, d], drecv.at[t, d])
        for d in order:
            se[t, d] = se[t, d] + rd[t, d]
        for d in far:
            go(se.at[t, d], re.at[t, d], esend.at[t, d], erecv.at[t, d], 2 * chip(d) + c)

    def finish(t):
        for d in range(1, nx):
            landed(se.at[t, d], re.at[t, d], esend.at[t, d], erecv.at[t, d])
        out_ref[t * chunk:(t + 1) * chunk, pl.ds(pl.multiple_of(me * wide, wide), wide)] = (
            se[t, 0] + sum(re[t, d] for d in range(1, nx))).astype(BF16)
        for d in far:
            go(out_at(t, me), out_at(t, me), fsend.at[t, d], frecv.at[t, d], 2 * chip(d) + c)
        go(out_at(t, me), out_at(t, me), gsend.at[t, 0], grecv.at[t, 0], partner)

    def forward(t):
        for d in near:
            src = 2 * chip(nx - d) + c
            landed(out_at(t, me), out_at(t, src), fsend.at[t, d], frecv.at[t, d])
            go(out_at(t, src), out_at(t, src), gsend.at[t, d], grecv.at[t, d], partner)

    local(0)
    pl.semaphore_wait(bar, len(peers))
    share(0)
    for t in range(1, chunks):
        local(t)
        share(t)
        pair(t - 1)
    for cp in wloads:
        cp.wait()
    project(0)
    pair(chunks - 1)
    for t in range(1, chunks):
        project(t)
        reduce(t - 1)
    reduce(chunks - 1)
    for t in range(chunks - 1):
        finish(t)
    forward(0)
    finish(chunks - 1)
    for t in range(1, chunks):
        forward(t)
    for t in range(chunks):
        for d in [0] + near:
            src = 2 * chip(nx - d if d else 0) + 1 - c
            landed(out_at(t, me), out_at(t, src), gsend.at[t, d], grecv.at[t, d])
    for cp in pending:
        cp.wait_send()


def solution(mesh):
    n = mesh.shape['sp']
    nx = n // 2
    row_spec = P(('rep', 'dp'), None)
    cache_spec = P(('rep', 'dp'), 'sp', None, None)
    len_spec = P(('rep', 'dp'))
    VM = pl.BlockSpec(memory_space=pltpu.VMEM)
    HB = pl.BlockSpec(memory_space=pltpu.HBM)
    SM = pl.BlockSpec(memory_space=pltpu.SMEM)
    DMA = pltpu.SemaphoreType.DMA

    def local_step(hidden, w_query, w_key, w_value, w_out, k_cache, v_cache, write_pos, valid_len):
        rows, seq, kv_heads, hd = k_cache.shape
        width = hidden.shape[1]
        proj = w_query.shape[1]
        heads = proj // hd
        cols = proj // n
        per = heads // n
        k3, v3 = k_cache.reshape(rows, seq, hd), v_cache.reshape(rows, seq, hd)
        sds = jax.ShapeDtypeStruct

        group, chunk = 8, rows // 4
        chunks = rows // chunk
        f = pltpu.VMEM
        q, kv, kb, vb = pl.pallas_call(
            functools.partial(qkv_kernel, n),
            out_shape=(f((n, rows, cols), BF16), sds((2, rows, hd), BF16),
                       f((rows, seq, hd), BF16), f((rows, seq, hd), BF16)),
            in_specs=[HB] * 6, out_specs=(VM,) * 4,
            scratch_shapes=[f((rows, width), BF16), f((2, width, cols), BF16), f((width, hd), BF16),
                            DMA, DMA((3,)), DMA((2, 4)), DMA((2, 2)), DMA((2, 2)), DMA((3,)), DMA((3,))],
            compiler_params=pltpu.CompilerParams(collective_id=0, has_side_effects=True,
                                                 vmem_limit_bytes=46 * 2 ** 20),
            name='qkv',
        )(hidden, w_query, w_key, w_value, k3, v3)

        place = lax.axis_index('sp') * seq + jnp.arange(seq, dtype=jnp.int32)
        at_pos = (place[None, :] == write_pos[:, None])[:, :, None]
        k_new = jnp.where(at_pos, kv[0][:, None, :], kb)
        v_new = jnp.where(at_pos, kv[1][:, None, :], vb)

        halves = hd // LANES
        wide = width // n
        pair = (chunks, nx, halves, per * chunk, LANES)
        sums = (chunks, nx, chunk, wide)
        mls = (chunks, nx, 8, LANES)
        own = (chunks, halves, heads * chunk, LANES)
        out = pl.pallas_call(
            functools.partial(attn_out_kernel, n, group, hd ** -0.5),
            out_shape=sds((rows, width), BF16),
            in_specs=[SM, VM, VM, VM, HB], out_specs=VM,
            scratch_shapes=[f(own, F32), f(own, F32), f((chunks, n, 8, LANES), F32),
                            f((n, w_out.shape[0], wide), BF16),
                            f(pair, F32), f(mls, F32), f(pair, F32), f(mls, F32), f(pair, F32), f(mls, F32),
                            f(sums, F32), f(sums, F32), f(sums, F32), f(sums, F32),
                            DMA((n,))] + [DMA((chunks, nx))] * 16,
            cost_estimate=pl.CostEstimate(flops=30 * 10 ** 9, bytes_accessed=60 * 10 ** 6, transcendentals=0),
            compiler_params=pltpu.CompilerParams(collective_id=1, has_side_effects=True,
                                                 vmem_limit_bytes=20 * 2 ** 20),
            name='attn_out',
        )(valid_len, q, k_new, v_new, pltpu.with_memory_space_constraint(w_out, pltpu.HBM))
        return out, k_new.reshape(k_cache.shape), v_new.reshape(v_cache.shape)

    return jax.shard_map(local_step, mesh=mesh,
                         in_specs=(row_spec, P(), P(), P(), P('sp', None), cache_spec, cache_spec, len_spec, len_spec),
                         out_specs=(row_spec, cache_spec, cache_spec), check_vma=False)
```

time: 45.9 us -> 46.8 us (1.020)
  other arithmetic: 0 us -> 3.55 us
  Pallas kernels: 44.3 us -> 40.8 us
  local copies, waits for them, and re-layouts: 0.8 us -> 1.59 us
    pallas_call x2 -> x1, Pallas kernels: 33.1 us -> 29 us  [local_step(): pl.pallas_call(functools.partial(attn_out_kernel, n, group, hd ** (-0.5))...]
    select_n x0 -> x1, other arithmetic: none -> 2.82 us  [local_step(): v_new = jnp.where(at_pos, kv[1][:, None, :], vb)]
    broadcast_in_dim x0 -> x1, local copies, waits for them, and re-layouts: none -> 0.78 us  [local_step(): v_new = jnp.where(at_pos, kv[1][:, None, :], vb)]
    eq x0 -> x1, other arithmetic: none -> 0.73 us  [local_step(): at_pos = (place[None, :] == write_pos[:, None])[:, :, None]]
    pallas_call x1, Pallas kernels: 11.2 us -> 11.8 us  [local_step(): pl.pallas_call(functools.partial(qkv_kernel, n), out_shape=(f((n, rows, c...]
where the time goes in v4:
time: 46.8 us; the launch traced here: 46.6 us
  Pallas kernels  40.8 us (87%)
  other arithmetic  3.55 us (8%)
  local copies, waits for them, and re-layouts  1.59 us (3%)
  between operations  0.71 us (2%)
    pallas_call x1, Pallas kernels, local_step(): pl.pallas_call(functools.partial(attn_out_kernel, n, group, hd ** (-0.5))...  29 us
    pallas_call x1, Pallas kernels, local_step(): pl.pallas_call(functools.partial(qkv_kernel, n), out_shape=(f((n, rows, c...  11.8 us
    select_n x1, other arithmetic, local_step(): v_new = jnp.where(at_pos, kv[1][:, None, :], vb)  2.82 us

profile of v4, /device:TPU:97, one launch (start us, length us, event | category | flops | bytes accessed | tf_op | source)
XLA Modules:
  0.0 46.6 jit_solution(8193248331667915922)
XLA Ops:
  0.6 0.7 %broadcast_compare_fusion = pred[64,256]{1,0:T(8,128)(4,1)S(1)} fusion(s32[256]{0:T(256)S(1)} %iota_add_fusion, s32[64]{0:T(128)} %param.16), kind=kLoop, calls=%fused_computation.4 | loop fusion | flops 16384 | bytes 17664 | tf_op jit(solution)/shard_map/eq | solution.py:334
  1.4 11.8 %qkv.1 = (bf16[8,64,512]{2,1,0:T(8,128)(2,1)S(1)}, bf16[2,64,256]{2,1,0:T(8,128)(2,1)}, bf16[64,256,256]{2,1,0:T(8,128)(2,1)S(1)}, bf16[64,256,256]{2,1,0:T(8,128)(2,1)S(1)}) custom-call(bf16[64,4096]{1,0:T(8,128)(2,1)} %hid_hbm.1, bf16[4096,4096]{1,0:T(8,128)(2,1)} %wq_hbm.1, bf16[4096,256]{1,0:T(8,128)(2,1)} %wk_hbm.1, bf16[4096,256]{1,0:T(8,128)(2,1)} %wv_hbm.1, ...), custom_call_target="tpu_custom_call" | custom-call | tf_op jit(solution)/shard_map/qkv/pallas_call | solution.py:321
  13.2 0.8 %slice_bitcast_fusion = (bf16[64,256]{1,0:T(8,128)(2,1)S(1)}, bf16[64,256]{1,0:T(8,128)(2,1)S(1)}) fusion(bf16[2,64,256]{2,1,0:T(8,128)(2,1)} %get-tuple-element.8), kind=kLoop, calls=%fused_computation.2 | loop fusion | bytes 131072 | tf_op jit(solution)/shard_map/jit(_where)/broadcast_in_dim | solution.py:336
  14.0 0.0 copy-start.2
  14.0 2.8 %broadcast_select_fusion = (bf16[64,256,256]{2,1,0:T(8,128)(2,1)S(1)}, bf16[64,256,256]{2,1,0:T(8,128)(2,1)S(1)}) fusion(bf16[64,256,256]{2,1,0:T(8,128)(2,1)S(1)} %get-tuple-element.10, pred[64,256]{1,0:T(8,128)(4,1)S(1)} %broadcast_compare_fusion, bf16[64,256]{1,0:T(8,128)(2,1)S(1)} %get-tuple-element.14, bf16[64,256,256]{2,1,0:T(8,128)(2,1)S(1)} %get-tuple-element.9, ...), kind=kLoop, calls=%fused_computation | loop fusion | flops 8388608 | bytes 33636352 | tf_op jit(solution)/shard_map/jit(_where)/select_n | solution.py:336
  16.8 0.0 copy-start
  16.8 0.0 copy-start.1
  16.8 0.0 copy-done.2
  16.8 29.0 %attn_out.1 = bf16[64,4096]{1,0:T(8,128)(2,1)S(1)} custom-call(s32[64]{0:T(128)S(1)} %copy-done.2, bf16[8,64,512]{2,1,0:T(8,128)(2,1)S(1)} %get-tuple-element.7.q_ref, bf16[64,256,256]{2,1,0:T(8,128)(2,1)S(1)} %get-tuple-element.17.kb, bf16[64,256,256]{2,1,0:T(8,128)(2,1)S(1)} %get-tuple-element.16.vb, bf16[512,4096]{1,0:T(8,128)(2,1)} %w_hbm.1), custom_call_target="tpu_custom_call" | custom-call | flops 30000001024 | bytes 60000000 | tf_op jit(solution)/shard_map/attn_out/pallas_call | solution.py:344
  45.8 0.0 copy-done
  45.8 0.0 copy-done.1
  45.9 0.8 %copy.15 = bf16[64,4096]{1,0:T(8,128)(2,1)} copy(bf16[64,4096]{1,0:T(8,128)(2,1)S(1)} %attn_out.1) | data formatting | bytes 1048576
  (1 shorter events, 0.0 us)
Async XLA Ops:
  14.0 2.9 %copy-start.2 = (s32[64]{0:T(128)S(1)}, s32[64]{0:T(128)}, u32[]{:S(2)}) copy-start(s32[64]{0:T(128)} %vl.1) | copy-start | bytes 772
  16.8 29.0 %copy-start = (bf16[64,256,256]{2,1,0:T(8,128)(2,1)}, bf16[64,256,256]{2,1,0:T(8,128)(2,1)S(1)}, u32[]{:S(2)}) copy-start(bf16[64,256,256]{2,1,0:T(8,128)(2,1)S(1)} %get-tuple-element.16.vb) | copy-start | bytes 25165828
  16.8 29.0 %copy-start.1 = (bf16[64,256,256]{2,1,0:T(8,128)(2,1)}, bf16[64,256,256]{2,1,0:T(8,128)(2,1)S(1)}, u32[]{:S(2)}) copy-start(bf16[64,256,256]{2,1,0:T(8,128)(2,1)S(1)} %get-tuple-element.17.kb) | copy-start | bytes 25165828

commit v5 on v4

--- a/solution.py
+++ b/solution.py
@@ -23,8 +23,9 @@
                                         device_id=sp_dev(dev), device_id_type=MESH)
 
 
-def qkv_kernel(n, hid_hbm, wq_hbm, wk_hbm, wv_hbm, k_hbm, v_hbm, q_ref, kv_ref, kb, vb,
-               hid, wq, wkv, hsem, wsem, csem, ssem, rsem, psend, precv):
+def qkv_kernel(n, group, chunk, scale, hid_hbm, wq_hbm, wk_hbm, wv_hbm, k_hbm, v_hbm, wp_hbm, vl_hbm,
+               q_ref, kv_ref, kb, vb, acc, ml, hid, wq, wkv, qs, kvs, wp, vl, hsem, wsem, csem, isem, ssem, rsem, psend,
+               precv):
     nx = n // 2
     me = lax.axis_index('sp')
     x, c = me // 2, lax.rem(me, 2)
@@ -39,6 +40,9 @@
         cp = pltpu.make_async_copy(wq_hbm.at[:, pl.ds(pl.multiple_of(blk * cols, cols), cols)], wq.at[i], wsem.at[i])
         cp.start()
         loads.append(cp)
+    ints = [pltpu.make_async_copy(src, dst, isem.at[i]) for i, (src, dst) in enumerate(((wp_hbm, wp), (vl_hbm, vl)))]
+    for cp in ints:
+        cp.start()
     near = [lax.rem(x + d, nx) for d in (1, nx - 1)]
     bar = pltpu.get_barrier_semaphore()
     peers = [2 * t + u for t in near for u in range(2)] + [partner]
@@ -89,7 +93,11 @@
     for d in range(2):
         for t in range(2):
             rcopy(q_ref.at[own], q_ref.at[2 * near[1 - d] + t], ssem.at[d, t], rsem.at[d, t], partner).wait_recv()
-    for cp in caches:
+    for cp in ints + caches[:2]:
+        cp.wait()
+    kvs[...] = kv_ref[:, 0:chunk, :].astype(F32)
+    attend_chunk(qs, q_ref, kb, vb, vl, acc, ml, 0, group, chunk, me * kb.shape[1], scale, (wp, kvs))
+    for cp in caches[2:]:
         cp.wait()
 
 
@@ -101,7 +109,7 @@
             qs[z, h * chunk:(h + 1) * chunk, :] = q_ref[h // per, t * chunk:(t + 1) * chunk, lo:lo + LANES].astype(F32)
 
 
-def attend(qs, kb, vb, vl, acc, b0, at0, group, chunk, heads, base, scale, m_all, l_all):
+def attend(qs, kb, vb, vl, acc, b0, at0, group, chunk, heads, base, scale, m_all, l_all, fresh=None):
     seq, hd = kb.shape[1:]
     halves = hd // LANES
     pos_iota = lax.broadcasted_iota(jnp.int32, (heads, seq), 1)
@@ -111,34 +119,63 @@
         qb = jnp.concatenate([qs[z, pl.ds(at0 + r, heads, stride=chunk), :] for z in range(halves)], axis=1)
         scores.append(lax.dot_general(qb.astype(BF16), kb[b0 + at0 + r], (((1,), (1,)), ((), ())),
                                       preferred_element_type=F32))
-    probs = []
+    probs, extra = [], []
     for r in range(group):
         valid = pos_iota < vl[b0 + at0 + r] - base
-        s = jnp.where(valid, scores[r] * scale, NEG)
+        s = scores[r]
+        if fresh is not None:
+            wp, kvs = fresh
+            newest = pos_iota == wp[b0 + at0 + r] - base
+            qb = jnp.concatenate([qs[z, pl.ds(at0 + r, heads, stride=chunk), :] for z in range(halves)], axis=1)
+            s = jnp.where(newest, jnp.sum(qb * kvs[0, pl.ds(at0 + r, 1), :], axis=1, keepdims=True), s)
+        s = jnp.where(valid, s * scale, NEG)
         m = jnp.max(s, axis=1, keepdims=True)
         p = jnp.where(valid, jnp.exp(s - m), 0.0)
         l = jnp.sum(p, axis=1, keepdims=True)
         here = lane_iota == at0 + r
         m_all = jnp.where(here, m, m_all)
         l_all = jnp.where(here, l, l_all)
-        probs.append(p.astype(BF16))
+        p = p.astype(BF16)
+        if fresh is not None:
+            p = p.astype(F32)
+            extra.append(jnp.sum(jnp.where(newest, p, 0.0), axis=1, keepdims=True) * kvs[1, pl.ds(at0 + r, 1), :])
+            p = jnp.where(newest, 0.0, p).astype(BF16)
+        probs.append(p)
     for r in range(group):
         o = jnp.dot(probs[r], vb[b0 + at0 + r], preferred_element_type=F32)
+        if fresh is not None:
+            o = o + extra[r]
         for z in range(halves):
             acc[z, pl.ds(at0 + r, heads, stride=chunk), :] = o[:, z * LANES:(z + 1) * LANES]
     return m_all, l_all
 
 
-def attn_out_kernel(n, group, scale, vl, q_ref, kb, vb, w_hbm, out_ref, qs, acc, ml, wv,
+def attend_chunk(qs, q_ref, kb, vb, vl, acc, ml, t, group, chunk, base, scale, fresh=None):
+    n, hd = q_ref.shape[0], kb.shape[2]
+    per = q_ref.shape[2] // hd
+    heads = n * per
+    stage_q(qs, q_ref, t, chunk, hd)
+
+    def step(g, carry):
+        return attend(qs, kb, vb, vl, acc, t * chunk, g * group, group, chunk, heads, base, scale, *carry, fresh)
+
+    init = (jnp.full((heads, LANES), NEG, F32), jnp.zeros((heads, LANES), F32))
+    m_all, l_all = lax.fori_loop(0, chunk // group, step, init)
+    for i in range(n):
+        ml[i, 0:per, :] = m_all[i * per:(i + 1) * per]
+        ml[i, per:2 * per, :] = l_all[i * per:(i + 1) * per]
+
+
+def attn_out_kernel(n, group, scale, vl_hbm, q_ref, kb, vb, acc0, ml0, w_ref, out_ref, qs, acc, ml, vl, vsem,
                     ra, rml, sb, sml, rb, rbml, sd, rd, se, re,
-                    wsem, amsend, amrecv, bmsend, bmrecv, asend, arecv, bsend, brecv, dsend, drecv, esend, erecv,
+                    amsend, amrecv, bmsend, bmrecv, asend, arecv, bsend, brecv, dsend, drecv, esend, erecv,
                     fsend, frecv, gsend, grecv):
     nx = n // 2
     me = lax.axis_index('sp')
     x, c = me // 2, lax.rem(me, 2)
     partner = 2 * x + 1 - c
     wide = out_ref.shape[1] // n
-    chunks, halves = acc.shape[:2]
+    chunks, halves = acc.shape[0] + 1, acc.shape[1]
     blk = acc.shape[2] // n
     chunk = out_ref.shape[0] // chunks
     per = blk // chunk
@@ -152,14 +189,14 @@
         return lax.rem(x + d, nx)
 
     bar = pltpu.get_barrier_semaphore()
-    peers = [2 * chip(d) + c for d in range(1, nx)] + [partner]
+    peers = [2 * chip(d) + u for d in range(1, nx) for u in range(2)] + [partner]
     for peer in peers:
         pl.semaphore_signal(bar, inc=1, device_id=sp_dev(peer), device_id_type=MESH)
-    wloads = []
-    for j in range(n):
-        cp = pltpu.make_async_copy(w_hbm.at[:, j * wide:(j + 1) * wide], wv.at[j], wsem.at[j])
-        cp.start()
-        wloads.append(cp)
+    lens = pltpu.make_async_copy(vl_hbm, vl, vsem)
+    lens.start()
+
+    def w_at(j):
+        return w_ref[:, pl.ds(pl.multiple_of(j * wide, wide), wide)]
 
     pending = []
 
@@ -175,31 +212,27 @@
         return pl.multiple_of(j * blk, blk)
 
     def local(t):
-        stage_q(qs.at[t], q_ref, t, chunk, hd)
-
-        def step(g, carry):
-            return attend(qs.at[t], kb, vb, vl, acc.at[t], t * chunk, g * group, group, chunk, heads,
-                          me * kb.shape[1], scale, *carry)
-
-        init = (jnp.full((heads, LANES), NEG, F32), jnp.zeros((heads, LANES), F32))
-        m_all, l_all = lax.fori_loop(0, chunk // group, step, init)
-        for i in range(n):
-            ml[t, i, 0:per, :] = m_all[i * per:(i + 1) * per]
-            ml[t, i, per:2 * per, :] = l_all[i * per:(i + 1) * per]
+        attend_chunk(qs.at[t - 1], q_ref, kb, vb, vl, acc.at[t - 1], ml.at[t - 1], t, group, chunk, me * kb.shape[1], scale)
+
+    def acc_of(t):
+        return acc.at[t - 1] if t else acc0
+
+    def ml_of(t):
+        return ml.at[t - 1] if t else ml0
 
     def share(t):
         for d in order:
             j = 2 * chip(d) + 1 - c
-            go(ml.at[t, j], rml.at[t, d], amsend.at[t, d], amrecv.at[t, d], partner)
-            go(acc.at[t, :, pl.ds(acc_at(j), blk)], ra.at[t, d], asend.at[t, d], arecv.at[t, d], partner)
+            go(ml_of(t).at[j], rml.at[t, d], amsend.at[t, d], amrecv.at[t, d], partner)
+            go(acc_of(t).at[:, pl.ds(acc_at(j), blk)], ra.at[t, d], asend.at[t, d], arecv.at[t, d], partner)
 
     def pair(t):
         for d in order:
-            landed(ml.at[t, 0], rml.at[t, d], amsend.at[t, d], amrecv.at[t, d])
+            landed(ml_of(t).at[0], rml.at[t, d], amsend.at[t, d], amrecv.at[t, d])
             landed(ra.at[t, d], ra.at[t, d], asend.at[t, d], arecv.at[t, d])
         for d in order:
             j = 2 * chip(d) + c
-            mine, theirs = ml[t, j], rml[t, d]
+            mine, theirs = ml_of(t)[j], rml[t, d]
             m = jnp.maximum(mine[0:per], theirs[0:per])
             fa, fb = jnp.exp(mine[0:per] - m), jnp.exp(theirs[0:per] - m)
             l = fa * mine[per:2 * per] + fb * theirs[per:2 * per]
@@ -209,7 +242,7 @@
             for h in range(per):
                 r = slice(h * chunk, (h + 1) * chunk)
                 for z in range(halves):
-                    own = acc[t, z, pl.ds(acc_at(j) + h * chunk, chunk), :]
+                    own = acc_of(t)[z, pl.ds(acc_at(j) + h * chunk, chunk), :]
                     sb[t, d, z, r, :] = own * f[:, h:h + 1] + ra[t, d, z, r, :] * f[:, per + h:per + h + 1]
         for d in far:
             j = 2 * chip(d) + c
@@ -236,11 +269,11 @@
                 parts.append(sum(u * f[:, d * per + h:d * per + h + 1] for d, u in enumerate(terms)))
         attn = jnp.concatenate(parts, axis=1).astype(BF16)
         for d in order:
-            sd[t, d] = jnp.dot(attn, wv[2 * chip(d) + 1 - c], preferred_element_type=F32)
+            sd[t, d] = jnp.dot(attn, w_at(2 * chip(d) + 1 - c), preferred_element_type=F32)
         for d in order:
             go(sd.at[t, d], rd.at[t, d], dsend.at[t, d], drecv.at[t, d], partner)
         for d in order:
-            se[t, d] = jnp.dot(attn, wv[2 * chip(d) + c], preferred_element_type=F32)
+            se[t, d] = jnp.dot(attn, w_at(2 * chip(d) + c), preferred_element_type=F32)
 
     def reduce(t):
         for d in order:
@@ -255,36 +288,39 @@
             landed(se.at[t, d], re.at[t, d], esend.at[t, d], erecv.at[t, d])
         out_ref[t * chunk:(t + 1) * chunk, pl.ds(pl.multiple_of(me * wide, wide), wide)] = (
             se[t, 0] + sum(re[t, d] for d in range(1, nx))).astype(BF16)
+        last = t == chunks - 1
         for d in far:
             go(out_at(t, me), out_at(t, me), fsend.at[t, d], frecv.at[t, d], 2 * chip(d) + c)
+            if last:
+                go(out_at(t, me), out_at(t, me), gsend.at[t, d], grecv.at[t, d], 2 * chip(d) + 1 - c)
         go(out_at(t, me), out_at(t, me), gsend.at[t, 0], grecv.at[t, 0], partner)
 
     def forward(t):
         for d in near:
             src = 2 * chip(nx - d) + c
             landed(out_at(t, me), out_at(t, src), fsend.at[t, d], frecv.at[t, d])
-            go(out_at(t, src), out_at(t, src), gsend.at[t, d], grecv.at[t, d], partner)
-
-    local(0)
+            if t < chunks - 1:
+                go(out_at(t, src), out_at(t, src), gsend.at[t, d], grecv.at[t, d], partner)
+
     pl.semaphore_wait(bar, len(peers))
     share(0)
-    for t in range(1, chunks):
+    lens.wait()
+    local(1)
+    share(1)
+    pair(0)
+    for t in range(2, chunks):
         local(t)
         share(t)
         pair(t - 1)
-    for cp in wloads:
-        cp.wait()
     project(0)
     pair(chunks - 1)
+    reduce(0)
     for t in range(1, chunks):
         project(t)
-        reduce(t - 1)
-    reduce(chunks - 1)
-    for t in range(chunks - 1):
+        reduce(t)
+    for t in range(chunks):
         finish(t)
-    forward(0)
-    finish(chunks - 1)
-    for t in range(1, chunks):
+    for t in range(chunks):
         forward(t)
     for t in range(chunks):
         for d in [0] + near:
@@ -318,43 +354,48 @@
         group, chunk = 8, rows // 4
         chunks = rows // chunk
         f = pltpu.VMEM
-        q, kv, kb, vb = pl.pallas_call(
-            functools.partial(qkv_kernel, n),
-            out_shape=(f((n, rows, cols), BF16), sds((2, rows, hd), BF16),
-                       f((rows, seq, hd), BF16), f((rows, seq, hd), BF16)),
-            in_specs=[HB] * 6, out_specs=(VM,) * 4,
+        halves = hd // LANES
+        own = (halves, heads * chunk, LANES)
+        hbm = [pltpu.with_memory_space_constraint(u, pltpu.HBM)
+               for u in (hidden, w_query, w_key, w_value, k3, v3, write_pos, valid_len)]
+        q, kv, kb, vb, acc0, ml0 = pl.pallas_call(
+            functools.partial(qkv_kernel, n, group, chunk, hd ** -0.5),
+            out_shape=(f((n, rows, cols), BF16), f((2, rows, hd), BF16),
+                       f((rows, seq, hd), BF16), f((rows, seq, hd), BF16), f(own, F32), f((n, 2 * per, LANES), F32)),
+            in_specs=[HB] * 8, out_specs=(VM,) * 6,
             scratch_shapes=[f((rows, width), BF16), f((2, width, cols), BF16), f((width, hd), BF16),
-                            DMA, DMA((3,)), DMA((2, 4)), DMA((2, 2)), DMA((2, 2)), DMA((3,)), DMA((3,))],
+                            f(own, F32), f((2, chunk, hd), F32), pltpu.SMEM((rows,), jnp.int32),
+                            pltpu.SMEM((rows,), jnp.int32),
+                            DMA, DMA((3,)), DMA((2, chunks)), DMA((2,)), DMA((2, 2)), DMA((2, 2)), DMA((3,)), DMA((3,))],
             compiler_params=pltpu.CompilerParams(collective_id=0, has_side_effects=True,
-                                                 vmem_limit_bytes=46 * 2 ** 20),
+                                                 vmem_limit_bytes=24 * 2 ** 20),
             name='qkv',
-        )(hidden, w_query, w_key, w_value, k3, v3)
-
+        )(*hbm)
+
+        kv, when = lax.optimization_barrier((kv, write_pos))
         place = lax.axis_index('sp') * seq + jnp.arange(seq, dtype=jnp.int32)
-        at_pos = (place[None, :] == write_pos[:, None])[:, :, None]
+        at_pos = (place[None, :] == when[:, None])[:, :, None]
         k_new = jnp.where(at_pos, kv[0][:, None, :], kb)
         v_new = jnp.where(at_pos, kv[1][:, None, :], vb)
 
-        halves = hd // LANES
         wide = width // n
         pair = (chunks, nx, halves, per * chunk, LANES)
         sums = (chunks, nx, chunk, wide)
-        mls = (chunks, nx, 8, LANES)
-        own = (chunks, halves, heads * chunk, LANES)
+        mls = (chunks, nx, 2 * per, LANES)
+        own = (chunks - 1,) + own
         out = pl.pallas_call(
             functools.partial(attn_out_kernel, n, group, hd ** -0.5),
             out_shape=sds((rows, width), BF16),
-            in_specs=[SM, VM, VM, VM, HB], out_specs=VM,
-            scratch_shapes=[f(own, F32), f(own, F32), f((chunks, n, 8, LANES), F32),
-                            f((n, w_out.shape[0], wide), BF16),
+            in_specs=[HB, VM, VM, VM, VM, VM, VM], out_specs=VM,
+            scratch_shapes=[f(own, F32), f(own, F32), f((chunks - 1, n, 2 * per, LANES), F32), pltpu.SMEM((rows,), jnp.int32), DMA,
                             f(pair, F32), f(mls, F32), f(pair, F32), f(mls, F32), f(pair, F32), f(mls, F32),
                             f(sums, F32), f(sums, F32), f(sums, F32), f(sums, F32),
-                            DMA((n,))] + [DMA((chunks, nx))] * 16,
+                            ] + [DMA((chunks, nx))] * 16,
             cost_estimate=pl.CostEstimate(flops=30 * 10 ** 9, bytes_accessed=60 * 10 ** 6, transcendentals=0),
             compiler_params=pltpu.CompilerParams(collective_id=1, has_side_effects=True,
                                                  vmem_limit_bytes=20 * 2 ** 20),
             name='attn_out',
-        )(valid_len, q, k_new, v_new, pltpu.with_memory_space_constraint(w_out, pltpu.HBM))
+        )(hbm[-1], q, k_new, v_new, acc0, ml0, w_out)
         return out, k_new.reshape(k_cache.shape), v_new.reshape(v_cache.shape)
 
     return jax.shard_map(local_step, mesh=mesh,

time: 46.8 us -> 41.8 us (0.89)
  Pallas kernels: 40.8 us -> 37.3 us
  local copies, waits for them, and re-layouts: 1.59 us -> 0.83 us
  other arithmetic: 3.55 us -> 2.91 us
    pallas_call x1, Pallas kernels: 29 us -> 24.8 us  [local_step(): pl.pallas_call(functools.partial(attn_out_kernel, n, group, hd ** (-0.5))...]
    broadcast_in_dim x1, local copies, waits for them, and re-layouts: 0.78 us -> 0.01 us  [local_step(): v_new = jnp.where(at_pos, kv[1][:, None, :], vb)]
    eq x1, other arithmetic: 0.73 us -> 0.08 us  [local_step(): at_pos = (place[None, :] == when[:, None])[:, :, None]]
    pallas_call x1, Pallas kernels: 11.8 us -> 12.4 us  [local_step(): pl.pallas_call(functools.partial(qkv_kernel, n, group, chunk, hd ** (-0.5...]
where the time goes in v5:
time: 41.8 us; the launch traced here: 41.7 us
  Pallas kernels  37.3 us (89%)
  other arithmetic  2.91 us (7%)
  local copies, waits for them, and re-layouts  0.83 us (2%)
  between operations  0.74 us (2%)
    pallas_call x1, Pallas kernels, local_step(): pl.pallas_call(functools.partial(attn_out_kernel, n, group, hd ** (-0.5))...  24.8 us
    pallas_call x1, Pallas kernels, local_step(): pl.pallas_call(functools.partial(qkv_kernel, n, group, chunk, hd ** (-0.5...  12.4 us
    select_n x1, other arithmetic, local_step(): v_new = jnp.where(at_pos, kv[1][:, None, :], vb)  2.83 us

profile of v5, /device:TPU:97, one launch (start us, length us, event | category | flops | bytes accessed | tf_op | source)
XLA Modules:
  0.0 41.7 jit_solution(17194318671213087486)
XLA Ops:
  0.6 0.0 copy-start.3
  0.7 12.4 %qkv.1 = (bf16[8,64,512]{2,1,0:T(8,128)(2,1)S(1)}, bf16[2,64,256]{2,1,0:T(8,128)(2,1)S(1)}, bf16[64,256,256]{2,1,0:T(8,128)(2,1)S(1)}, bf16[64,256,256]{2,1,0:T(...) custom-call(bf16[64,4096]{1,0:T(8,128)(2,1)} %hid_hbm.1, bf16[4096,4096]{1,0:T(8,128)(2,1)} %wq_hbm.1, ...), custom_call_target="tpu_custom_call" | custom-call | tf_op jit(solution)/shard_map/qkv/pallas_call | solution.py:361
  13.1 0.0 copy-done.3
  13.1 0.1 broadcast_compare_fusion
  13.2 0.0 copy-start.2
  13.2 2.8 %broadcast_select_fusion = (bf16[64,256,256]{2,1,0:T(8,128)(2,1)S(1)}, bf16[64,256,256]{2,1,0:T(8,128)(2,1)S(1)}) fusion(bf16[64,256,256]{2,1,0:T(8,128)(2,1)S(1)} %get-tuple-element.16, pred[64,256]{1,0:T(8,128)(4,1)S(1)} %broadcast_compare_fusion, bf16[64,256]{1,0:T(8,128)(2,1)S(1)} %get-tuple-element.22, bf16[64,256,256]{2,1,0:T(8,128)(2,1)S(1)} %get-tuple-element.15, ...), kind=kLoop, calls=%fused_computation | loop fusion | flops 8388608 | bytes 33636352 | tf_op jit(solution)/shard_map/jit(_where)/select_n | solution.py:379
  16.0 0.0 copy-start
  16.1 0.0 copy-start.1
  16.1 0.0 copy-done.2
  16.1 24.8 %attn_out.1 = bf16[64,4096]{1,0:T(8,128)(2,1)S(1)} custom-call(s32[64]{0:T(128)} %vl_hbm.3, bf16[8,64,512]{2,1,0:T(8,128)(2,1)S(1)} %get-tuple-element.11.q_ref, bf16[64,256,256]{2,1,0:T(8,128)(2,1)S(1)} %get-tuple-element.25.kb, bf16[64,256,256]{2,1,0:T(8,128)(2,1)S(1)} %get-tuple-element.24.vb, f32[2,256,128]{2,1,0:T(8,128)S(1)} %get-tuple-element.17.acc0, ...), custom_call_target="tpu_custom_call" | custom-call | flops 30000001024 | bytes 60000000 | tf_op jit(solution)/shard_map/attn_out/pallas_call | solution.py:386
  40.9 0.0 copy-done
  40.9 0.0 copy-done.1
  40.9 0.8 %copy.15 = bf16[64,4096]{1,0:T(8,128)(2,1)} copy(bf16[64,4096]{1,0:T(8,128)(2,1)S(1)} %attn_out.1) | data formatting | bytes 1048576
  (2 shorter events, 0.0 us)
Async XLA Ops:
  0.6 12.4 %copy-start.3 = (s32[64]{0:T(128)S(1)}, s32[64]{0:T(128)}, u32[]{:S(2)}) copy-start(s32[64]{0:T(128)} %wp_hbm.1) | copy-start | bytes 772
  13.2 2.9 %copy-start.2 = (bf16[512,4096]{1,0:T(8,128)(2,1)S(1)}, bf16[512,4096]{1,0:T(8,128)(2,1)}, u32[]{:S(2)}) copy-start(bf16[512,4096]{1,0:T(8,128)(2,1)} %w_ref.1) | copy-start | bytes 12582916
  16.0 24.9 %copy-start = (bf16[64,256,256]{2,1,0:T(8,128)(2,1)}, bf16[64,256,256]{2,1,0:T(8,128)(2,1)S(1)}, u32[]{:S(2)}) copy-start(bf16[64,256,256]{2,1,0:T(8,128)(2,1)S(1)} %get-tuple-element.24.vb) | copy-start | bytes 25165828
  16.1 24.9 %copy-start.1 = (bf16[64,256,256]{2,1,0:T(8,128)(2,1)}, bf16[64,256,256]{2,1,0:T(8,128)(2,1)S(1)}, u32[]{:S(2)}) copy-start(bf16[64,256,256]{2,1,0:T(8,128)(2,1)S(1)} %get-tuple-element.25.kb) | copy-start | bytes 25165828

commit v6 on v5

--- a/solution.py
+++ b/solution.py
@@ -24,8 +24,8 @@
 
 
 def qkv_kernel(n, group, chunk, scale, hid_hbm, wq_hbm, wk_hbm, wv_hbm, k_hbm, v_hbm, wp_hbm, vl_hbm,
-               q_ref, kv_ref, kb, vb, acc, ml, hid, wq, wkv, qs, kvs, wp, vl, hsem, wsem, csem, isem, ssem, rsem, psend,
-               precv):
+               q_ref, kv_ref, kb, vb, acc, ml, ra, rml, hid, wq, wkv, qs, kvs, wp, vl, hsem, wsem, csem, isem, ssem, rsem, psend,
+               precv, asend, arecv, msend, mrecv):
     nx = n // 2
     me = lax.axis_index('sp')
     x, c = me // 2, lax.rem(me, 2)
@@ -36,8 +36,10 @@
     ch = pltpu.make_async_copy(hid_hbm, hid, hsem)
     ch.start()
     loads = []
-    for i, blk in enumerate((own, opp)):
-        cp = pltpu.make_async_copy(wq_hbm.at[:, pl.ds(pl.multiple_of(blk * cols, cols), cols)], wq.at[i], wsem.at[i])
+    half = cols // 2
+    for i, (blk, lo, size) in enumerate(((own, 0, half), (own, half, half), (opp, 0, cols))):
+        cp = pltpu.make_async_copy(wq_hbm.at[:, pl.ds(pl.multiple_of(blk * cols + lo, half), size)],
+                                   wq.at[i // 2, :, lo:lo + size], wsem.at[i])
         cp.start()
         loads.append(cp)
     ints = [pltpu.make_async_copy(src, dst, isem.at[i]) for i, (src, dst) in enumerate(((wp_hbm, wp), (vl_hbm, vl)))]
@@ -48,13 +50,32 @@
     peers = [2 * t + u for t in near for u in range(2)] + [partner]
     for peer in peers:
         pl.semaphore_signal(bar, inc=1, device_id=sp_dev(peer), device_id_type=MESH)
-    pick = [pltpu.make_async_copy(w, wkv, wsem.at[2]) for w in (wk_hbm, wv_hbm)]
+    pick = [pltpu.make_async_copy(w, wkv, wsem.at[3]) for w in (wk_hbm, wv_hbm)]
     for i in range(2):
         @pl.when(c == i)
         def _():
             pick[i].start()
+
+    def project(w):
+        return jnp.dot(hid[...], w, preferred_element_type=F32).astype(BF16)
+
+    def part(blk, h):
+        return q_ref.at[blk, :, h * half:(h + 1) * half]
+
+    sends = []
+
+    def go(*args):
+        sends.append(rcopy(*args))
+        sends[-1].start()
+
     ch.wait()
     loads[0].wait()
+    q_ref[own, :, 0:half] = project(wq[0, :, 0:half])
+    pl.semaphore_wait(bar, len(peers))
+    for d in range(2):
+        go(part(own, 0), part(own, 0), ssem.at[d, 0], rsem.at[d, 0], 2 * near[d] + c)
+    go(part(own, 0), part(own, 0), psend.at[0], precv.at[0], partner)
+    loads[1].wait()
     parts = csem.shape[1]
     step = kb.shape[0] // parts
     caches = []
@@ -63,42 +84,50 @@
             cp = pltpu.make_async_copy(src.at[pl.ds(g * step, step)], dst.at[pl.ds(g * step, step)], csem.at[i, g])
             cp.start()
             caches.append(cp)
-
-    def project(w):
-        return jnp.dot(hid[...], w, preferred_element_type=F32).astype(BF16)
-
-    q_ref[own] = project(wq[0])
-    pl.semaphore_wait(bar, len(peers))
-    sends = []
+    q_ref[own, :, half:cols] = project(wq[0, :, half:cols])
     for d in range(2):
         for t in range(2):
-            sends.append(rcopy(q_ref.at[own], q_ref.at[own], ssem.at[d, t], rsem.at[d, c], 2 * near[d] + t))
-    sends.append(rcopy(q_ref.at[own], q_ref.at[own], psend.at[0], precv.at[0], partner))
-    for s in sends:
-        s.start()
-    loads[1].wait()
+            go(part(own, 1), part(own, 1), ssem.at[d, 1 + t], rsem.at[d, 1 + c], 2 * near[d] + t)
+    go(part(own, 1), part(own, 1), psend.at[1], precv.at[1], partner)
+    loads[2].wait()
     q_ref[opp] = project(wq[1])
-    sends.append(rcopy(q_ref.at[opp], q_ref.at[opp], psend.at[1], precv.at[1], partner))
-    sends[-1].start()
+    go(q_ref.at[opp], q_ref.at[opp], psend.at[2], precv.at[2], partner)
     pick[0].wait()
     kv_ref[c] = project(wkv[...])
-    sends.append(rcopy(kv_ref.at[c], kv_ref.at[c], psend.at[2], precv.at[2], partner))
-    sends[-1].start()
-    for s in sends:
-        s.wait_send()
+    go(kv_ref.at[c], kv_ref.at[c], psend.at[3], precv.at[3], partner)
+    for d in range(2):
+        blk = 2 * near[1 - d] + c
+        rcopy(part(own, 0), part(blk, 0), ssem.at[d, 0], rsem.at[d, 0], partner).wait_recv()
+        go(part(blk, 0), part(blk, 0), psend.at[4 + d], precv.at[4 + d], partner)
     popp = 2 * lax.rem(x + nx // 2, nx) + 1 - c
-    rcopy(q_ref.at[own], q_ref.at[partner], psend.at[0], precv.at[0], partner).wait_recv()
-    rcopy(q_ref.at[own], q_ref.at[popp], psend.at[1], precv.at[1], partner).wait_recv()
-    rcopy(kv_ref.at[c], kv_ref.at[1 - c], psend.at[2], precv.at[2], partner).wait_recv()
+    for h in range(2):
+        rcopy(part(own, h), part(partner, h), psend.at[h], precv.at[h], partner).wait_recv()
+    rcopy(q_ref.at[own], q_ref.at[popp], psend.at[2], precv.at[2], partner).wait_recv()
+    rcopy(kv_ref.at[c], kv_ref.at[1 - c], psend.at[3], precv.at[3], partner).wait_recv()
     for d in range(2):
         for t in range(2):
-            rcopy(q_ref.at[own], q_ref.at[2 * near[1 - d] + t], ssem.at[d, t], rsem.at[d, t], partner).wait_recv()
+            rcopy(part(own, 1), part(2 * near[1 - d] + t, 1), ssem.at[d, 1 + t], rsem.at[d, 1 + t],
+                  partner).wait_recv()
+        rcopy(part(own, 0), part(2 * near[1 - d] + 1 - c, 0), psend.at[4 + d], precv.at[4 + d], partner).wait_recv()
     for cp in ints + caches[:2]:
         cp.wait()
     kvs[...] = kv_ref[:, 0:chunk, :].astype(F32)
     attend_chunk(qs, q_ref, kb, vb, vl, acc, ml, 0, group, chunk, me * kb.shape[1], scale, (wp, kvs))
+    blk = ra.shape[2]
+    handed = []
+    for d in range(nx):
+        j = 2 * lax.rem(x + d, nx) + 1 - c
+        handed.append(rcopy(ml.at[j], rml.at[d], msend.at[d], mrecv.at[d], partner))
+        handed.append(rcopy(acc.at[:, pl.ds(pl.multiple_of(j * blk, blk), blk)], ra.at[d], asend.at[d], arecv.at[d],
+                            partner))
+    for cp in handed:
+        cp.start()
     for cp in caches[2:]:
         cp.wait()
+    for cp in handed:
+        cp.wait()
+    for cp in sends:
+        cp.wait_send()
 
 
 def stage_q(qs, q_ref, t, chunk, hd):
@@ -166,7 +195,7 @@
         ml[i, per:2 * per, :] = l_all[i * per:(i + 1) * per]
 
 
-def attn_out_kernel(n, group, scale, vl_hbm, q_ref, kb, vb, acc0, ml0, w_ref, out_ref, qs, acc, ml, vl, vsem,
+def attn_out_kernel(n, group, scale, vl_hbm, q_ref, kb, vb, acc0, ml0, ra0, rml0, w_ref, out_ref, qs, acc, ml, vl, vsem,
                     ra, rml, sb, sml, rb, rbml, sd, rd, se, re,
                     amsend, amrecv, bmsend, bmrecv, asend, arecv, bsend, brecv, dsend, drecv, esend, erecv,
                     fsend, frecv, gsend, grecv):
@@ -226,13 +255,14 @@
             go(ml_of(t).at[j], rml.at[t, d], amsend.at[t, d], amrecv.at[t, d], partner)
             go(acc_of(t).at[:, pl.ds(acc_at(j), blk)], ra.at[t, d], asend.at[t, d], arecv.at[t, d], partner)
 
-    def pair(t):
-        for d in order:
+    def merge(t):
+        got, got_ml = (ra.at[t], rml.at[t]) if t else (ra0, rml0)
+        for d in order if t else ():
             landed(ml_of(t).at[0], rml.at[t, d], amsend.at[t, d], amrecv.at[t, d])
             landed(ra.at[t, d], ra.at[t, d], asend.at[t, d], arecv.at[t, d])
         for d in order:
             j = 2 * chip(d) + c
-            mine, theirs = ml_of(t)[j], rml[t, d]
+            mine, theirs = ml_of(t)[j], got_ml[d]
             m = jnp.maximum(mine[0:per], theirs[0:per])
             fa, fb = jnp.exp(mine[0:per] - m), jnp.exp(theirs[0:per] - m)
             l = fa * mine[per:2 * per] + fb * theirs[per:2 * per]
@@ -243,11 +273,17 @@
                 r = slice(h * chunk, (h + 1) * chunk)
                 for z in range(halves):
                     own = acc_of(t)[z, pl.ds(acc_at(j) + h * chunk, chunk), :]
-                    sb[t, d, z, r, :] = own * f[:, h:h + 1] + ra[t, d, z, r, :] * f[:, per + h:per + h + 1]
+                    sb[t, d, z, r, :] = own * f[:, h:h + 1] + got[d, z, r, :] * f[:, per + h:per + h + 1]
+
+    def spread(t):
         for d in far:
             j = 2 * chip(d) + c
             go(sml.at[t, d], rbml.at[t, d], bmsend.at[t, d], bmrecv.at[t, d], j)
             go(sb.at[t, d], rb.at[t, d], bsend.at[t, d], brecv.at[t, d], j)
+
+    def pair(t):
+        merge(t)
+        spread(t)
 
     def out_at(t, j):
         return out_ref.at[pl.ds(t * chunk, chunk), pl.ds(pl.multiple_of(j * wide, wide), wide)]
@@ -302,12 +338,12 @@
             if t < chunks - 1:
                 go(out_at(t, src), out_at(t, src), gsend.at[t, d], grecv.at[t, d], partner)
 
-    pl.semaphore_wait(bar, len(peers))
-    share(0)
+    merge(0)
     lens.wait()
     local(1)
+    pl.semaphore_wait(bar, len(peers))
+    spread(0)
     share(1)
-    pair(0)
     for t in range(2, chunks):
         local(t)
         share(t)
@@ -358,15 +394,16 @@
         own = (halves, heads * chunk, LANES)
         hbm = [pltpu.with_memory_space_constraint(u, pltpu.HBM)
                for u in (hidden, w_query, w_key, w_value, k3, v3, write_pos, valid_len)]
-        q, kv, kb, vb, acc0, ml0 = pl.pallas_call(
+        q, kv, kb, vb, acc0, ml0, ra0, rml0 = pl.pallas_call(
             functools.partial(qkv_kernel, n, group, chunk, hd ** -0.5),
             out_shape=(f((n, rows, cols), BF16), f((2, rows, hd), BF16),
-                       f((rows, seq, hd), BF16), f((rows, seq, hd), BF16), f(own, F32), f((n, 2 * per, LANES), F32)),
-            in_specs=[HB] * 8, out_specs=(VM,) * 6,
+                       f((rows, seq, hd), BF16), f((rows, seq, hd), BF16), f(own, F32), f((n, 2 * per, LANES), F32),
+                       f((nx, halves, per * chunk, LANES), F32), f((nx, 2 * per, LANES), F32)),
+            in_specs=[HB] * 8, out_specs=(VM,) * 8,
             scratch_shapes=[f((rows, width), BF16), f((2, width, cols), BF16), f((width, hd), BF16),
                             f(own, F32), f((2, chunk, hd), F32), pltpu.SMEM((rows,), jnp.int32),
                             pltpu.SMEM((rows,), jnp.int32),
-                            DMA, DMA((3,)), DMA((2, chunks)), DMA((2,)), DMA((2, 2)), DMA((2, 2)), DMA((3,)), DMA((3,))],
+                            DMA, DMA((4,)), DMA((2, chunks)), DMA((2,)), DMA((2, 3)), DMA((2, 3)), DMA((6,)), DMA((6,))] + [DMA((nx,))] * 4,
             compiler_params=pltpu.CompilerParams(collective_id=0, has_side_effects=True,
                                                  vmem_limit_bytes=24 * 2 ** 20),
             name='qkv',
@@ -386,7 +423,7 @@
         out = pl.pallas_call(
             functools.partial(attn_out_kernel, n, group, hd ** -0.5),
             out_shape=sds((rows, width), BF16),
-            in_specs=[HB, VM, VM, VM, VM, VM, VM], out_specs=VM,
+            in_specs=[HB, VM, VM, VM, VM, VM, VM, VM, VM], out_specs=VM,
             scratch_shapes=[f(own, F32), f(own, F32), f((chunks - 1, n, 2 * per, LANES), F32), pltpu.SMEM((rows,), jnp.int32), DMA,
                             f(pair, F32), f(mls, F32), f(pair, F32), f(mls, F32), f(pair, F32), f(mls, F32),
                             f(sums, F32), f(sums, F32), f(sums, F32), f(sums, F32),
@@ -395,7 +432,7 @@
             compiler_params=pltpu.CompilerParams(collective_id=1, has_side_effects=True,
                                                  vmem_limit_bytes=20 * 2 ** 20),
             name='attn_out',
-        )(hbm[-1], q, k_new, v_new, acc0, ml0, w_out)
+        )(hbm[-1], q, k_new, v_new, acc0, ml0, ra0, rml0, w_out)
         return out, k_new.reshape(k_cache.shape), v_new.reshape(v_cache.shape)
 
     return jax.shard_map(local_step, mesh=mesh,

time: 41.8 us -> 40.8 us (0.976)
  Pallas kernels: 37.3 us -> 36.3 us
    pallas_call x1, Pallas kernels: 24.8 us -> 23.7 us  [local_step(): pl.pallas_call(functools.partial(attn_out_kernel, n, group, hd ** (-0.5))...]
where the time goes in v6:
time: 40.8 us; the launch traced here: 40.7 us
  Pallas kernels  36.3 us (89%)
  other arithmetic  2.91 us (7%)
  local copies, waits for them, and re-layouts  0.83 us (2%)
  between operations  0.74 us (2%)
    pallas_call x1, Pallas kernels, local_step(): pl.pallas_call(functools.partial(attn_out_kernel, n, group, hd ** (-0.5))...  23.7 us
    pallas_call x1, Pallas kernels, local_step(): pl.pallas_call(functools.partial(qkv_kernel, n, group, chunk, hd ** (-0.5...  12.6 us
    select_n x1, other arithmetic, local_step(): v_new = jnp.where(at_pos, kv[1][:, None, :], vb)  2.83 us
    unnamed x9, local copies, waits for them, and re-layouts  0.82 us

profile of v6, /device:TPU:97, one launch (start us, length us, event | category | flops | bytes accessed | tf_op | source)
XLA Modules:
  0.0 40.7 jit_solution(11442563672726264968)
XLA Ops:
  0.6 0.0 copy-start.3
  0.7 12.6 %qkv.1 = (bf16[8,64,512]{2,1,0:T(8,128)(2,1)S(1)}, bf16[2,64,256]{2,1,0:T(8,128)(2,1)S(1)}, bf16[64,256,256]{2,1,0:T(8,128)(2,1)S(1)}, bf16[64,256,256]{2,1,0:T(...) custom-call(bf16[64,4096]{1,0:T(8,128)(2,1)} %hid_hbm.1, ...), custom_call_target="tpu_custom_call" | custom-call | tf_op jit(solution)/shard_map/qkv/pallas_call | solution.py:397
  13.2 0.0 copy-done.3
  13.2 0.1 broadcast_compare_fusion
  13.3 0.0 copy-start.2
  13.3 2.8 %broadcast_select_fusion = (bf16[64,256,256]{2,1,0:T(8,128)(2,1)S(1)}, bf16[64,256,256]{2,1,0:T(8,128)(2,1)S(1)}) fusion(bf16[64,256,256]{2,1,0:T(8,128)(2,1)S(1)} %get-tuple-element.18, pred[64,256]{1,0:T(8,128)(4,1)S(1)} %broadcast_compare_fusion, bf16[64,256]{1,0:T(8,128)(2,1)S(1)} %get-tuple-element.26, bf16[64,256,256]{2,1,0:T(8,128)(2,1)S(1)} %get-tuple-element.17, ...), kind=kLoop, calls=%fused_computation | loop fusion | flops 8388608 | bytes 33636352 | tf_op jit(solution)/shard_map/jit(_where)/select_n | solution.py:416
  16.2 0.0 copy-start
  16.2 0.0 copy-start.1
  16.2 0.0 copy-done.2
  16.2 23.7 %attn_out.1 = bf16[64,4096]{1,0:T(8,128)(2,1)S(1)} custom-call(s32[64]{0:T(128)} %vl_hbm.3, bf16[8,64,512]{2,1,0:T(8,128)(2,1)S(1)} %get-tuple-element.13.q_ref, bf16[64,256,256]{2,1,0:T(8,128)(2,1)S(1)} %get-tuple-element.29.kb, bf16[64,256,256]{2,1,0:T(8,128)(2,1)S(1)} %get-tuple-element.28.vb, f32[2,256,128]{2,1,0:T(8,128)S(1)} %get-tuple-element.19.acc0, ...), custom_call_target="tpu_custom_call" | custom-call | flops 30000001024 | bytes 60000000 | tf_op jit(solution)/shard_map/attn_out/pallas_call | solution.py:423
  39.9 0.0 copy-done
  39.9 0.0 copy-done.1
  39.9 0.8 %copy.15 = bf16[64,4096]{1,0:T(8,128)(2,1)} copy(bf16[64,4096]{1,0:T(8,128)(2,1)S(1)} %attn_out.1) | data formatting | bytes 1048576
  (2 shorter events, 0.0 us)
Async XLA Ops:
  0.6 12.6 %copy-start.3 = (s32[64]{0:T(128)S(1)}, s32[64]{0:T(128)}, u32[]{:S(2)}) copy-start(s32[64]{0:T(128)} %wp_hbm.1) | copy-start | bytes 772
  13.3 2.9 %copy-start.2 = (bf16[512,4096]{1,0:T(8,128)(2,1)S(1)}, bf16[512,4096]{1,0:T(8,128)(2,1)}, u32[]{:S(2)}) copy-start(bf16[512,4096]{1,0:T(8,128)(2,1)} %w_ref.1) | copy-start | bytes 12582916
  16.2 23.7 %copy-start = (bf16[64,256,256]{2,1,0:T(8,128)(2,1)}, bf16[64,256,256]{2,1,0:T(8,128)(2,1)S(1)}, u32[]{:S(2)}) copy-start(bf16[64,256,256]{2,1,0:T(8,128)(2,1)S(1)} %get-tuple-element.28.vb) | copy-start | bytes 25165828
  16.2 23.7 %copy-start.1 = (bf16[64,256,256]{2,1,0:T(8,128)(2,1)}, bf16[64,256,256]{2,1,0:T(8,128)(2,1)S(1)}, u32[]{:S(2)}) copy-start(bf16[64,256,256]{2,1,0:T(8,128)(2,1)S(1)} %get-tuple-element.29.kb) | copy-start | bytes 25165828

commit v7 on v6

--- a/solution.py
+++ b/solution.py
@@ -354,7 +354,11 @@
     for t in range(1, chunks):
         project(t)
         reduce(t)
+    sent = len(pending)
     for t in range(chunks):
+        if t == chunks - 1:
+            for cp in pending[:sent]:
+                cp.wait_send()
         finish(t)
     for t in range(chunks):
         forward(t)
@@ -362,7 +366,7 @@
         for d in [0] + near:
             src = 2 * chip(nx - d if d else 0) + 1 - c
             landed(out_at(t, me), out_at(t, src), gsend.at[t, d], grecv.at[t, d])
-    for cp in pending:
+    for cp in pending[sent:]:
         cp.wait_send()
 
 

time: 40.8 us -> 40.7 us (level)
  no operation moved by 1% of the time
where the time goes in v7:
time: 40.7 us; the launch traced here: 40.6 us
  Pallas kernels  36.1 us (89%)
  other arithmetic  2.91 us (7%)
  local copies, waits for them, and re-layouts  0.83 us (2%)
  between operations  0.74 us (2%)
    pallas_call x1, Pallas kernels, local_step(): pl.pallas_call(functools.partial(attn_out_kernel, n, group, hd ** (-0.5))...  23.6 us
    pallas_call x1, Pallas kernels, local_step(): pl.pallas_call(functools.partial(qkv_kernel, n, group, chunk, hd ** (-0.5...  12.6 us
    select_n x1, other arithmetic, local_step(): v_new = jnp.where(at_pos, kv[1][:, None, :], vb)  2.83 us
    unnamed x9, local copies, waits for them, and re-layouts  0.82 us

profile of v7, /device:TPU:97, one launch (start us, length us, event | category | flops | bytes accessed | tf_op | source)
XLA Modules:
  0.0 40.6 jit_solution(3708604763929702934)
XLA Ops:
  0.6 0.0 copy-start.3
  0.7 12.6 %qkv.1 = (bf16[8,64,512]{2,1,0:T(8,128)(2,1)S(1)}, bf16[2,64,256]{2,1,0:T(8,128)(2,1)S(1)}, bf16[64,256,256]{2,1,0:T(8,128)(2,1)S(1)}, bf16[64,256,256]{2,1,0:T(...) custom-call(bf16[64,4096]{1,0:T(8,128)(2,1)} %hid_hbm.1, ...), custom_call_target="tpu_custom_call" | custom-call | tf_op jit(solution)/shard_map/qkv/pallas_call | solution.py:401
  13.2 0.0 copy-done.3
  13.2 0.1 broadcast_compare_fusion
  13.3 0.0 copy-start.2
  13.3 2.8 %broadcast_select_fusion = (bf16[64,256,256]{2,1,0:T(8,128)(2,1)S(1)}, bf16[64,256,256]{2,1,0:T(8,128)(2,1)S(1)}) fusion(bf16[64,256,256]{2,1,0:T(8,128)(2,1)S(1)} %get-tuple-element.18, pred[64,256]{1,0:T(8,128)(4,1)S(1)} %broadcast_compare_fusion, bf16[64,256]{1,0:T(8,128)(2,1)S(1)} %get-tuple-element.26, bf16[64,256,256]{2,1,0:T(8,128)(2,1)S(1)} %get-tuple-element.17, ...), kind=kLoop, calls=%fused_computation | loop fusion | flops 8388608 | bytes 33636352 | tf_op jit(solution)/shard_map/jit(_where)/select_n | solution.py:420
  16.2 0.0 copy-start
  16.2 0.0 copy-start.1
  16.2 0.0 copy-done.2
  16.2 23.6 %attn_out.1 = bf16[64,4096]{1,0:T(8,128)(2,1)S(1)} custom-call(s32[64]{0:T(128)} %vl_hbm.3, bf16[8,64,512]{2,1,0:T(8,128)(2,1)S(1)} %get-tuple-element.13.q_ref, bf16[64,256,256]{2,1,0:T(8,128)(2,1)S(1)} %get-tuple-element.29.kb, bf16[64,256,256]{2,1,0:T(8,128)(2,1)S(1)} %get-tuple-element.28.vb, f32[2,256,128]{2,1,0:T(8,128)S(1)} %get-tuple-element.19.acc0, ...), custom_call_target="tpu_custom_call" | custom-call | flops 30000001024 | bytes 60000000 | tf_op jit(solution)/shard_map/attn_out/pallas_call | solution.py:427
  39.8 0.0 copy-done
  39.8 0.0 copy-done.1
  39.8 0.8 %copy.15 = bf16[64,4096]{1,0:T(8,128)(2,1)} copy(bf16[64,4096]{1,0:T(8,128)(2,1)S(1)} %attn_out.1) | data formatting | bytes 1048576
  (2 shorter events, 0.0 us)
Async XLA Ops:
  0.6 12.6 %copy-start.3 = (s32[64]{0:T(128)S(1)}, s32[64]{0:T(128)}, u32[]{:S(2)}) copy-start(s32[64]{0:T(128)} %wp_hbm.1) | copy-start | bytes 772
  13.3 2.9 %copy-start.2 = (bf16[512,4096]{1,0:T(8,128)(2,1)S(1)}, bf16[512,4096]{1,0:T(8,128)(2,1)}, u32[]{:S(2)}) copy-start(bf16[512,4096]{1,0:T(8,128)(2,1)} %w_ref.1) | copy-start | bytes 12582916
  16.2 23.6 %copy-start = (bf16[64,256,256]{2,1,0:T(8,128)(2,1)}, bf16[64,256,256]{2,1,0:T(8,128)(2,1)S(1)}, u32[]{:S(2)}) copy-start(bf16[64,256,256]{2,1,0:T(8,128)(2,1)S(1)} %get-tuple-element.28.vb) | copy-start | bytes 25165828
  16.2 23.6 %copy-start.1 = (bf16[64,256,256]{2,1,0:T(8,128)(2,1)}, bf16[64,256,256]{2,1,0:T(8,128)(2,1)S(1)}, u32[]{:S(2)}) copy-start(bf16[64,256,256]{2,1,0:T(8,128)(2,1)S(1)} %get-tuple-element.29.kb) | copy-start | bytes 25165828
